TPU v7x, 32 devices: a whole 2x2x4 slice. The times are simulated.
32 devices in a mesh: wide: 8 (over z, y), narrow: 4 (over x, core).
Axes of the slice: x: 2, y: 2, z: 4, core: 2. Of those that a mesh axis runs over, the one named last changes fastest.
Arguments:
- inputs: bfloat16 [16384, 1024], P('wide', 'narrow'), may hold values from -6 to 6
- cotangent: bfloat16 [16384, 1024], P('wide', 'narrow'), may hold values from -6 to 6
- routing: int32 [16384], replicated, may hold values from 0 to 16383, as said below
- lengths: int32 [8, 4], P('wide'), may hold values from 1 to 1024, 2048 in all within a row
- ln1_gain: float32 [1024], P('narrow'), may hold values from 0.1 to 1.9
- ln1_bias: float32 [1024], P('narrow'), may hold values from -1.5 to 1.5
- qkv_weight: float32 [1024, 3, 1024], P('wide', None, 'narrow'), may hold values from -0.1875 to 0.1875
- qv_bias: float32 [2, 1024], P(None, 'narrow'), may hold values from -1.5 to 1.5
- out_weight: float32 [1024, 1024], P('narrow', 'wide'), may hold values from -1.5 to 1.5
- out_bias: float32 [1024], P('narrow'), may hold values from -1.5 to 1.5
- ln2_gain: float32 [1024], P('narrow'), may hold values from 0.1 to 1.9
- ln2_bias: float32 [1024], P('narrow'), may hold values from -1.5 to 1.5
- up_weight: float32 [1024, 4096], P('wide', 'narrow'), may hold values from -0.1875 to 0.1875
- up_bias: float32 [4096], P('narrow'), may hold values from -1.5 to 1.5
- down_weight: float32 [4096, 1024], P('narrow', 'wide'), may hold values from -0.09375 to 0.09375
- down_bias: float32 [1024], P('narrow'), may hold values from -1.5 to 1.5
Outputs:
- outputs: bfloat16 [16384, 1024], P('wide', 'narrow')
- input_grad: bfloat16 [16384, 1024], P('wide', 'narrow')
- ln1_gain_grad: float32 [1024], P('narrow')
- ln1_bias_grad: float32 [1024], P('narrow')
- qkv_weight_grad: float32 [1024, 3, 1024], P('wide', None, 'narrow')
- qv_bias_grad: float32 [2, 1024], P(None, 'narrow')
- out_weight_grad: float32 [1024, 1024], P('narrow', 'wide')
- out_bias_grad: float32 [1024], P('narrow')
- ln2_gain_grad: float32 [1024], P('narrow')
- ln2_bias_grad: float32 [1024], P('narrow')
- up_weight_grad: float32 [1024, 4096], P('wide', 'narrow')
- up_bias_grad: float32 [4096], P('narrow')
- down_weight_grad: float32 [4096, 1024], P('narrow', 'wide')
- down_bias_grad: float32 [1024], P('narrow')
Inputs may be any that keep to these rules, and one draw needn't show every extreme that they name: routing is a permutation of the 16384 input rows; each aligned block of 2048 positions takes exactly 256 rows from each aligned block of 2048 input rows. Row w gives, in order, the lengths of the documents that fill positions w * 2048 to (w + 1) * 2048 - 1 of the routed order; each row sums to 2048.
All inputs are finite; a program needn't handle non-finite values.
Results may differ from a plain program's by a relative error of at most 0.012.
The roundings to bfloat16 on the way count: a program that leaves them out, or rounds other values in their place, can miss the bound.
Values may be sent and summed in bfloat16 or wider, within the bound.
A program may use at most 192 MiB of HBM per device.

v0:
```python
import jax
import jax.numpy as jnp
from jax import lax
from jax.sharding import PartitionSpec as P

D = 1024
HEAD_DIM = 64
SEQ_MAX = 1024


NORM_EPS = 1e-05


def split_up(shard, dim, length):
    dims = shard.shape
    parts = shard.reshape(*dims[:dim], length, dims[dim] // length, *dims[dim + 1 :])
    return jnp.moveaxis(parts, dim, 0)


def sent_and_summed(shard, axis, dim):
    length = lax.axis_size(axis)
    parts = lax.all_to_all(split_up(shard, dim, length), axis, 0, 0, tiled=True)
    return jnp.sum(parts.astype(jnp.float32), axis=0)


def in_one_piece(arrays, axis, dim, along):
    both = jnp.concatenate(arrays, axis=along)
    result, at, outs = (sent_and_summed(both, axis, dim), 0, [])
    for a in arrays:
        outs.append(lax.slice_in_dim(result, at, at + a.shape[along], axis=along))
        at += a.shape[along]
    return tuple(outs)


def row_totals(first, second):
    return lax.psum((first, second), "narrow")


def feature_gather(share_rows):
    return lax.all_gather(share_rows, "narrow", axis=1, tiled=True)


def partial_sums(partial_rows):
    return lax.psum_scatter(partial_rows, "narrow", scatter_dimension=1, tiled=True)


def share_norm(share_rows, gain_vec, shift_vec):
    totals = row_totals(jnp.sum(share_rows, axis=1), jnp.sum(share_rows * share_rows, axis=1))
    row_mean = totals[0] / D
    row_scale = lax.rsqrt(totals[1] / D - row_mean * row_mean + NORM_EPS)
    normed = (share_rows - row_mean[:, None]) * row_scale[:, None]
    return (normed * gain_vec + shift_vec, row_mean, row_scale)


def norm_back(grad_rows, share_rows, row_mean, row_scale, gain_vec):
    normed = (share_rows - row_mean[:, None]) * row_scale[:, None]
    scaled = grad_rows * gain_vec
    totals = row_totals(jnp.sum(scaled, axis=1), jnp.sum(scaled * normed, axis=1))
    back_rows = row_scale[:, None] * (
        scaled - totals[0][:, None] / D - normed * totals[1][:, None] / D
    )
    return (back_rows, jnp.sum(grad_rows * normed, axis=0), jnp.sum(grad_rows, axis=0))


def block_scores(queries, key_rows, segment, block_index, block_rows, key_span):
    row_count = queries.shape[0]
    block_start = block_index * block_rows
    key_start = jnp.clip(block_start + block_rows - key_span, 0, row_count - key_span)
    query_block = lax.dynamic_slice_in_dim(queries, block_start, block_rows, 0)
    key_block = lax.dynamic_slice_in_dim(key_rows, key_start, key_span, 0)
    scores = jnp.einsum(
        "qhd,khd->hqk", query_block, key_block, preferred_element_type=jnp.float32
    ) * HEAD_DIM ** (-0.5)
    query_pos = block_start + jnp.arange(block_rows, dtype=jnp.int32)
    key_pos = key_start + jnp.arange(key_span, dtype=jnp.int32)
    query_seg = lax.dynamic_slice_in_dim(segment, block_start, block_rows, 0)
    key_seg = lax.dynamic_slice_in_dim(segment, key_start, key_span, 0)
    allowed = (query_seg[:, None] == key_seg[None, :]) & (key_pos[None, :] <= query_pos[:, None])
    return (
        jnp.where(allowed[None], scores, -1000000000.0),
        query_block,
        key_block,
        block_start,
        key_start,
    )


def attention_forward(queries, key_rows, values, segment):
    row_count = queries.shape[0]
    block_rows = min(512, row_count)
    key_span = min(row_count, SEQ_MAX + block_rows)

    def one_block(block_index):
        scores, query_block, key_block, block_start, key_start = block_scores(
            queries, key_rows, segment, block_index, block_rows, key_span
        )
        value_block = lax.dynamic_slice_in_dim(values, key_start, key_span, 0)
        row_top = jnp.max(scores, axis=2, keepdims=True)
        weights = jnp.exp(scores - row_top)
        denominator = jnp.sum(weights, axis=2, keepdims=True)
        attn_probs = (weights / denominator).astype(jnp.bfloat16)
        mixed_rows = jnp.einsum(
            "hqk,khd->qhd", attn_probs, value_block, preferred_element_type=jnp.float32
        )
        return (mixed_rows.astype(jnp.bfloat16), (row_top + jnp.log(denominator))[:, :, 0])

    mixed_rows, log_sums = lax.map(one_block, jnp.arange(row_count // block_rows, dtype=jnp.int32))
    return (mixed_rows.reshape(queries.shape), log_sums)


def attention_backward(queries, key_rows, values, grad_mixed, log_sums, segment):
    row_count = queries.shape[0]
    block_rows = min(512, row_count)
    key_span = min(row_count, SEQ_MAX + block_rows)
    head_scale = HEAD_DIM ** (-0.5)

    def one_block(carried, packed):
        key_grad, value_grad = carried
        block_index, block_sums = packed
        scores, query_block, key_block, block_start, key_start = block_scores(
            queries, key_rows, segment, block_index, block_rows, key_span
        )
        value_block = lax.dynamic_slice_in_dim(values, key_start, key_span, 0)
        grad_block = lax.dynamic_slice_in_dim(grad_mixed, block_start, block_rows, 0)
        attn_probs = jnp.exp(scores - block_sums[:, :, None])
        grad_probs = jnp.einsum(
            "qhd,khd->hqk", grad_block, value_block, preferred_element_type=jnp.float32
        )
        centre = jnp.sum(attn_probs * grad_probs, axis=2, keepdims=True)
        grad_scores = (attn_probs * (grad_probs - centre)).astype(jnp.bfloat16)
        query_grad = (
            jnp.einsum("hqk,khd->qhd", grad_scores, key_block, preferred_element_type=jnp.float32)
            * head_scale
        )
        key_part = (
            jnp.einsum("hqk,qhd->khd", grad_scores, query_block, preferred_element_type=jnp.float32)
            * head_scale
        )
        value_part = jnp.einsum(
            "hqk,qhd->khd",
            attn_probs.astype(jnp.bfloat16),
            grad_block,
            preferred_element_type=jnp.float32,
        )
        key_grad = lax.dynamic_update_slice_in_dim(
            key_grad,
            lax.dynamic_slice_in_dim(key_grad, key_start, key_span, 0) + key_part,
            key_start,
            0,
        )
        value_grad = lax.dynamic_update_slice_in_dim(
            value_grad,
            lax.dynamic_slice_in_dim(value_grad, key_start, key_span, 0) + value_part,
            key_start,
            0,
        )
        return ((key_grad, value_grad), query_grad)

    empty_grad = jnp.zeros(queries.shape, jnp.float32)
    block_count = row_count // block_rows
    (key_grad, value_grad), query_grad = lax.scan(
        one_block, (empty_grad, empty_grad), (jnp.arange(block_count, dtype=jnp.int32), log_sums)
    )
    return (query_grad.reshape(queries.shape), key_grad, value_grad)


def local(
    inputs,
    cotangent,
    routing,
    lengths,
    ln1_gain,
    ln1_bias,
    qkv_weight,
    qv_bias,
    out_weight,
    out_bias,
    ln2_gain,
    ln2_bias,
    up_weight,
    up_bias,
    down_weight,
    down_bias,
):
    row_count = inputs.shape[0]
    quarter = inputs.shape[1]
    heads_here = quarter // HEAD_DIM
    total_rows = routing.shape[0]
    row_base = lax.axis_index("wide") * row_count
    positions = jnp.arange(row_count, dtype=jnp.int32)
    routed_ids = lax.dynamic_slice_in_dim(routing, row_base, row_count, 0)
    arrange = jnp.argsort(routed_ids // row_count * row_count + positions)
    settle = jnp.argsort(arrange)
    inverse = (
        jnp.zeros((total_rows,), jnp.int32).at[routing].set(jnp.arange(total_rows, dtype=jnp.int32))
    )
    targets = lax.dynamic_slice_in_dim(inverse, row_base, row_count, 0)
    send_index = jnp.argsort(targets)
    return_index = jnp.argsort(send_index)
    arrived = (
        lax.all_to_all(inputs[send_index], "wide", split_axis=0, concat_axis=0, tiled=True),
        lax.all_to_all(cotangent[send_index], "wide", split_axis=0, concat_axis=0, tiled=True),
    )
    routed = arrived[0][settle]
    routed_grad = arrived[1][settle]
    routed_wide = routed.astype(jnp.float32)
    doc_ends = jnp.cumsum(lengths[0])
    segment = jnp.sum((positions[:, None] >= doc_ends[None, :]).astype(jnp.int32), axis=1)
    qkv_low = qkv_weight.astype(jnp.bfloat16).reshape(qkv_weight.shape[0], 3 * quarter)
    up_low = up_weight.astype(jnp.bfloat16)
    out_low = out_weight.astype(jnp.bfloat16)
    down_low = down_weight.astype(jnp.bfloat16)
    row_mats = (
        lax.all_gather(qkv_low, "wide", axis=0, tiled=True),
        lax.all_gather(up_low, "wide", axis=0, tiled=True),
    )
    col_mats = (
        lax.all_gather(out_low, "wide", axis=1, tiled=True),
        lax.all_gather(down_low, "wide", axis=1, tiled=True),
    )
    normed_one, mean_one, scale_one = share_norm(routed_wide, ln1_gain, ln1_bias)
    act_one = feature_gather(normed_one.astype(jnp.bfloat16))
    projected = jnp.dot(act_one, row_mats[0], preferred_element_type=jnp.float32).reshape(
        row_count, 3, quarter
    )
    no_shift = jnp.zeros((quarter,), jnp.float32)
    projected = (projected + jnp.stack([qv_bias[0], no_shift, qv_bias[1]])[None]).astype(
        jnp.bfloat16
    )
    head_shape = (row_count, heads_here, HEAD_DIM)
    queries = projected[:, 0].reshape(head_shape)
    key_rows = projected[:, 1].reshape(head_shape)
    values = projected[:, 2].reshape(head_shape)
    mixed_rows, log_sums = attention_forward(queries, key_rows, values, segment)
    attended = mixed_rows.reshape(row_count, quarter)
    partial_value = jnp.dot(attended, col_mats[0], preferred_element_type=jnp.float32)
    middle = routed_wide + partial_sums(partial_value) + out_bias
    normed_two, mean_two, scale_two = share_norm(middle, ln2_gain, ln2_bias)
    act_two = feature_gather(normed_two.astype(jnp.bfloat16))
    preact = jnp.dot(act_two, row_mats[1], preferred_element_type=jnp.float32) + up_bias
    hidden = jax.nn.gelu(preact, approximate=True).astype(jnp.bfloat16)
    result = (
        middle
        + partial_sums(jnp.dot(hidden, col_mats[1], preferred_element_type=jnp.float32))
        + down_bias
    )
    rows_back = (
        lax.all_gather(qkv_low, "wide", axis=0, tiled=True),
        lax.all_gather(up_low, "wide", axis=0, tiled=True),
    )
    cols_back = (
        lax.all_gather(out_low, "wide", axis=1, tiled=True),
        lax.all_gather(down_low, "wide", axis=1, tiled=True),
    )
    grad_full = feature_gather(routed_grad)
    down_grad = jnp.einsum("tf,td->fd", hidden, grad_full, preferred_element_type=jnp.float32)
    grad_hidden = jnp.einsum(
        "td,fd->tf", grad_full, cols_back[1], preferred_element_type=jnp.float32
    )
    _, gelu_back = jax.vjp(lambda preacts: jax.nn.gelu(preacts, approximate=True), preact)
    grad_pre = gelu_back(grad_hidden)[0].astype(jnp.bfloat16)
    up_grad = jnp.einsum("td,tf->df", act_two, grad_pre, preferred_element_type=jnp.float32)
    grad_act_two = partial_sums(
        jnp.einsum("tf,df->td", grad_pre, rows_back[1], preferred_element_type=jnp.float32)
    )
    back_two, gain_two_grad, shift_two_grad = norm_back(
        grad_act_two, middle, mean_two, scale_two, ln2_gain
    )
    grad_middle = routed_grad.astype(jnp.float32) + back_two
    grad_branch = grad_middle.astype(jnp.bfloat16)
    branch_full = feature_gather(grad_branch)
    out_grad = jnp.einsum("tf,td->fd", attended, branch_full, preferred_element_type=jnp.float32)
    grad_attended = jnp.einsum(
        "td,fd->tf", branch_full, cols_back[0], preferred_element_type=jnp.float32
    ).astype(jnp.bfloat16)
    query_grad, key_grad, value_grad = attention_backward(
        queries, key_rows, values, grad_attended.reshape(head_shape), log_sums, segment
    )
    grad_proj = jnp.stack(
        [
            query_grad.reshape(row_count, quarter),
            key_grad.reshape(row_count, quarter),
            value_grad.reshape(row_count, quarter),
        ],
        axis=1,
    ).astype(jnp.bfloat16)
    grad_flat = grad_proj.reshape(row_count, 3 * quarter)
    qkv_grad = jnp.einsum("td,tc->dc", act_one, grad_flat, preferred_element_type=jnp.float32)
    grad_act_one = partial_sums(
        jnp.einsum("tc,dc->td", grad_flat, rows_back[0], preferred_element_type=jnp.float32)
    )
    back_one, gain_one_grad, shift_one_grad = norm_back(
        grad_act_one, routed_wide, mean_one, scale_one, ln1_gain
    )
    grad_input = (grad_middle + back_one).astype(jnp.bfloat16)
    bias_pair = jnp.stack(
        [
            jnp.sum(grad_proj[:, 0], axis=0, dtype=jnp.float32),
            jnp.sum(grad_proj[:, 2], axis=0, dtype=jnp.float32),
        ]
    )
    small = lax.psum(
        (
            gain_one_grad,
            shift_one_grad,
            bias_pair,
            jnp.sum(grad_branch, axis=0, dtype=jnp.float32),
            gain_two_grad,
            shift_two_grad,
            jnp.sum(grad_pre, axis=0, dtype=jnp.float32),
            jnp.sum(routed_grad, axis=0, dtype=jnp.float32),
        ),
        "wide",
    )
    row_grads = in_one_piece(
        (qkv_grad.astype(jnp.bfloat16), up_grad.astype(jnp.bfloat16)), "wide", 0, 1
    )
    col_grads = in_one_piece(
        (out_grad.astype(jnp.bfloat16), down_grad.astype(jnp.bfloat16)), "wide", 1, 0
    )
    returned = (
        lax.all_to_all(
            result.astype(jnp.bfloat16)[arrange], "wide", split_axis=0, concat_axis=0, tiled=True
        ),
        lax.all_to_all(grad_input[arrange], "wide", split_axis=0, concat_axis=0, tiled=True),
    )
    return (
        returned[0][return_index],
        returned[1][return_index],
        small[0],
        small[1],
        row_grads[0].reshape(qkv_weight.shape),
        small[2],
        col_grads[0],
        small[3],
        small[4],
        small[5],
        row_grads[1],
        small[6],
        col_grads[1],
        small[7],
    )


def solution(mesh):
    placed = (
        P("wide", "narrow"),
        P("wide", "narrow"),
        P(),
        P("wide", None),
        P("narrow"),
        P("narrow"),
        P("wide", None, "narrow"),
        P(None, "narrow"),
        P("narrow", "wide"),
        P("narrow"),
        P("narrow"),
        P("narrow"),
        P("wide", "narrow"),
        P("narrow"),
        P("narrow", "wide"),
        P("narrow"),
    )
    return jax.shard_map(
        local,
        mesh=mesh,
        in_specs=placed,
        out_specs=(
            P("wide", "narrow"),
            P("wide", "narrow"),
            P("narrow"),
            P("narrow"),
            P("wide", None, "narrow"),
            P(None, "narrow"),
            P("narrow", "wide"),
            P("narrow"),
            P("narrow"),
            P("narrow"),
            P("wide", "narrow"),
            P("narrow"),
            P("narrow", "wide"),
            P("narrow"),
        ),
        check_vma=False,
    )
```

profile of v0, /device:TPU:0, one launch (start us, length us, event | category | flops | bytes accessed | tf_op | source)
XLA Modules:
  0.0 1251.2 jit_solution(571788685401750677)
XLA Ops:
  8.1 60.3 %scatter_custom_fusion = s32[16384]{0:T(1024)S(1)} fusion(s32[16384]{0:T(1024)S(1)} %compare_select_fusion, s32[16384]{0:T(1024)S(1)} %iota.72, s32[]{:T(128)} %constant.214.clone.1), kind=kCustom, calls=%fused_computation.119 | custom fusion | bytes 65540 | tf_op jit(solution)/shard_map/scatter | solution.py:195
  68.5 5.0 sort.59
  74.2 9.1 gather_fusion
  83.2 7.3 all-to-all-start
  92.2 5.0 sort.60
  97.3 5.0 sort.61
  102.3 20.3 %all-to-all-done = bf16[8,256,256]{2,1,0:T(8,128)(2,1)S(1)} async-done(((bf16[8,256,256]{2,1,0:T(8,128)(2,1)}), bf16[8,256,256]{2,1,0:T(8,128)(2,1)S(1)}, u32[]{:S(2)}, u32[]{:S(2)}) %all-to-all-start) | async-done | bytes 1048608 | tf_op jit(solution)/shard_map/all_to_all | solution.py:201
  122.7 7.5 gather_fusion.1
  130.8 10.8 all-reduce.4
  144.3 27.6 %all_gather.30 = bf16[256,1024]{1,0:T(8,128)(2,1)S(1)} all-gather(bf16[256,128]{1,0:T(8,128)(2,1)S(1)} %convert_element_type.132), channel_id=1, replica_groups=mesh['wide'=8,'narrow'=4] {'wide'}, dimensions={1}, use_global_device_ids=true | all-gather | bytes 589824 | tf_op jit(solution)/shard_map/all_gather | solution.py:218
  171.9 10.2 all-gather.9.cloned.1.call-done
  182.2 5.7 fusion.77
  189.9 62.9 %while.34 = (s32[]{:T(128)}, bf16[4,512,4,64]{1,3,2,0:T(8,128)(2,1)}, f32[4,4,512]{2,1,0:T(4,128)S(1)}, s32[4]{0:T(128)S(1)}, bf16[2048,4,64]{0,2,1:T(8,128)(2,1...) while((s32[]{:T(128)}, ...), condition=%wide.region_13.14_spmd, body=%wide.region_10.13_spmd.sunk | while | flops 845545472 | bytes 43098380 | solution.py:107
  199.5 6.1 fusion.125
  215.3 6.1 fusion.125
  231.0 6.1 fusion.125
  246.7 6.1 fusion.125
  263.1 69.3 %reduce-scatter.5.cloned.1.call-done = f32[2048,256]{1,0:T(8,128)} async-done(((f32[2048,1024]{1,0:T(8,128)}), f32[2048,256]{1,0:T(8,128)}) %reduce-scatter.5.cloned.1.call-update) | async-done | bytes 2097168 | tf_op jit(solution)/shard_map/reduce_scatter | solution.py:44
  335.6 10.3 all-reduce.3
  349.6 7.5 gather_fusion.4
  357.1 47.0 %all_to_all.58 = bf16[8,256,256]{2,1,0:T(8,128)(2,1)S(1)} all-to-all(bf16[8,256,256]{2,1,0:T(8,128)(2,1)S(1)} %bitcast.124), channel_id=1, replica_groups=mesh['wide'=8,'narrow'=4] {'wide'}, dimensions={0} | all-to-all | bytes 2097152 | tf_op jit(solution)/shard_map/all_to_all | solution.py:202
  404.1 9.0 gather_fusion.5
  413.1 23.9 %all-gather.13.cloned.1.call-done = bf16[2048,1024]{1,0:T(8,128)(2,1)} async-done(((bf16[2048,256]{1,0:T(8,128)(2,1)}), bf16[2048,1024]{1,0:T(8,128)(2,1)}) %all-gather.13.cloned.1.call-update) | async-done | bytes 4194320 | tf_op jit(solution)/shard_map/all_gather | solution.py:40
  437.1 10.6 fusion.79
  447.7 42.2 %all-gather.17.cloned.1.call-done = bf16[1024,1024]{1,0:T(8,128)(2,1)} async-done(((bf16[1024,128]{1,0:T(8,128)(2,1)}), bf16[1024,1024]{1,0:T(8,128)(2,1)}) %all-gather.17.cloned.1.call-update) | async-done | bytes 2097168 | tf_op jit(solution)/shard_map/all_gather | solution.py:219
  489.9 34.8 %all-gather.21.cloned.1.call-done = bf16[2048,1024]{1,0:T(8,128)(2,1)} async-done(((bf16[2048,256]{1,0:T(8,128)(2,1)}), bf16[2048,1024]{1,0:T(8,128)(2,1)}) %all-gather.21.cloned.1.call-update) | async-done | bytes 4194320 | tf_op jit(solution)/shard_map/all_gather | solution.py:40
  524.7 14.2 %convert_reduce_fusion = (f32[1024]{0:T(1024)}, bf16[2048,1024]{1,0:T(8,128)(2,1)S(1)}) fusion(f32[2048,1024]{1,0:T(8,128)} %fusion.79, f32[1024]{0:T(1024)S(1)} %copy-done.51, bf16[2048,1024]{1,0:T(8,128)(2,1)} %all-gather.21.cloned.1.call-done, bf16[1024,1024]{1,0:T(8,128)(2,1)} %all-gather.17.cloned.1.call-done), kind=kOutput, calls=%fused_computation.68 | convolution fusion | flops 4343200768 | bytes 18882560 | tf_op jit(solution)/shard_map/td,fd->tf/dot_general | solution.py:257
  541.0 7.0 fusion.80
  549.5 13.5 %fusion.71 = f32[2048,1024]{1,0:T(8,128)} fusion(bf16[1024,1024]{1,0:T(8,128)(2,1)S(1)} %copy-done.49, f32[2048,1024]{1,0:T(8,128)} %fusion.79, f32[1024]{0:T(1024)S(1)} %copy-done.51), kind=kOutput, calls=%fused_computation.146 | convolution fusion | flops 4315938816 | bytes 18878464 | tf_op jit(solution)/shard_map/dot_general | solution.py:244
  563.1 56.3 %reduce-scatter.9.cloned.1.call-done = f32[2048,256]{1,0:T(8,128)} async-done(((f32[2048,1024]{1,0:T(8,128)}), f32[2048,256]{1,0:T(8,128)}) %reduce-scatter.9.cloned.1.call-update) | async-done | bytes 2097168 | tf_op jit(solution)/shard_map/reduce_scatter | solution.py:44
  622.4 10.1 all-reduce.2
  632.6 60.6 %reduce-scatter.7.cloned.1.call-done = f32[2048,256]{1,0:T(8,128)} async-done(((f32[2048,1024]{1,0:T(8,128)}), f32[2048,256]{1,0:T(8,128)}) %reduce-scatter.7.cloned.1.call-update) | async-done | bytes 2097168 | tf_op jit(solution)/shard_map/reduce_scatter | solution.py:44
  693.2 6.4 convert_reduce_fusion.5
  699.7 35.1 %all-gather.19.cloned.1.call-done = bf16[2048,1024]{1,0:T(8,128)(2,1)} async-done(((bf16[2048,256]{1,0:T(8,128)(2,1)}), bf16[2048,1024]{1,0:T(8,128)(2,1)}) %all-gather.19.cloned.1.call-update) | async-done | bytes 4194320 | tf_op jit(solution)/shard_map/all_gather | solution.py:40
  742.5 222.9 %while.35 = (s32[]{:T(128)}, f32[2048,4,64]{0,2,1:T(8,128)}, f32[2048,4,64]{0,2,1:T(8,128)}, bf16[4,512,4,64]{1,0,3,2:T(4,128)(2,1)}, s32[4]{0:T(128)S(1)}, /*in...) while((s32[]{:T(128)}, f32[2048,4,64]{0,2,1:T(8,128)}, ...), condition=%wide.region_28.29_spmd, body=%wide.region_26.28_spmd.sunk | while | flops 2045378560 | bytes 153174416 | solution.py:161
  748.8 5.9 multiply_reduce_fusion.7
  769.2 10.2 dynamic_update_slice.59
  779.4 9.6 dynamic_update_slice.57
  789.0 9.6 dynamic_update_slice.58
  804.8 5.9 multiply_reduce_fusion.7
  825.1 10.2 dynamic_update_slice.59
  835.3 9.6 dynamic_update_slice.57
  845.0 9.6 dynamic_update_slice.58
  860.7 5.9 multiply_reduce_fusion.7
  881.1 10.2 dynamic_update_slice.59
  891.3 9.6 dynamic_update_slice.57
  900.9 9.6 dynamic_update_slice.58
  916.6 5.9 multiply_reduce_fusion.7
  936.9 10.2 dynamic_update_slice.59
  947.2 9.1 dynamic_update_slice.57
  956.3 9.1 dynamic_update_slice.58
  972.0 5.7 fusion.81
  978.9 9.0 gather_fusion.2
  988.0 5.5 all-to-all-start.1
  993.5 10.7 convolution_convert_fusion.1
  1007.5 12.2 all-to-all-done.1
  1024.4 8.4 convolution_convert_fusion.2
  1038.5 44.9 %all-to-all-done.5 = bf16[8,1280,128]{2,1,0:T(8,128)(2,1)} async-done(((bf16[8,1280,128]{2,1,0:T(8,128)(2,1)}), bf16[8,1280,128]{2,1,0:T(8,128)(2,1)}, u32[]{:S(2)}, u32[]{:S(2)}) %all-to-all-start.5) | async-done | bytes 2621472 | tf_op jit(solution)/shard_map/all_to_all | solution.py:22
  1090.6 10.9 all-reduce.1
  1105.3 9.1 gather_fusion.6
  1114.3 54.9 %all-to-all-done.4 = bf16[8,128,1792]{1,2,0:T(8,128)(2,1)} async-done(((bf16[8,128,1792]{1,2,0:T(8,128)(2,1)}), bf16[8,128,1792]{1,2,0:T(8,128)(2,1)}, u32[]{:S(2)}, u32[]{:S(2)}) %all-to-all-start.4) | async-done | bytes 3670048 | tf_op jit(solution)/shard_map/all_to_all | solution.py:22
  1178.3 9.0 gather_fusion.3
  1197.6 37.6 %all-reduce = (f32[256]{0:T(256)}, f32[256]{0:T(256)}, f32[2,256]{1,0:T(2,128)}, f32[256]{0:T(256)}, f32[256]{0:T(256)}, /*index=5*/f32[256]{0:T(256)}, f32[1024]{0:T(1024)}, f32[256]{0:T(256)}) all-reduce(f32[256]{0:T(256)S(1)} %get-tuple-element.451, ...), channel_id=1, replica_groups=mesh['wide'=8,'narrow'=4] {'wide'}, use_global_device_ids=true, to_apply=%region_35.36 | all-reduce | flops 3072 | bytes 24576 | tf_op jit(solution)/shard_map/psum | solution.py:302
  1235.1 9.1 gather_fusion.7
  (307 shorter events, 206.9 us)
Async XLA Ops:
  7.2 67.0 %copy-start = (bf16[2048,256]{1,0:T(8,128)(2,1)S(1)}, bf16[2048,256]{1,0:T(8,128)(2,1)}, u32[]{:S(2)}) copy-start(bf16[2048,256]{1,0:T(8,128)(2,1)} %param.20) | copy-start | bytes 3145732
  74.2 9.1 copy-start.25
  74.2 16.4 %copy-start.19 = (f32[128,3,256]{2,0,1:T(8,128)S(1)}, f32[128,3,256]{2,0,1:T(8,128)}, u32[]{:S(2)}) copy-start(f32[128,3,256]{2,0,1:T(8,128)} %param.26) | copy-start | bytes 1179652
  83.2 39.4 %all-to-all-start = ((bf16[8,256,256]{2,1,0:T(8,128)(2,1)}), bf16[8,256,256]{2,1,0:T(8,128)(2,1)S(1)}, u32[]{:S(2)}, u32[]{:S(2)}) async-start(bf16[8,256,256]{2,1,0:T(8,128)(2,1)} %bitcast.10), calls=%async_computation | async-start | bytes 2097152 | tf_op jit(solution)/shard_map/all_to_all | solution.py:201
  90.6 81.4 %all-gather.11.cloned.1.call-start = ((), (), s32[]{:S(2)}) async-start(), calls=%async_computation.11 | async-start | bytes 1769472 | tf_op jit(solution)/shard_map/all_gather | solution.py:214
  91.5 90.7 %all-gather.9.cloned.1.call-start = ((), (), s32[]{:S(2)}) async-start(), calls=%async_computation.10 | async-start | bytes 5242880 | tf_op jit(solution)/shard_map/all_gather | solution.py:40
  97.3 25.4 %copy-start.31 = (s32[2048]{0:T(1024)}, s32[2048]{0:T(1024)S(1)}, u32[]{:S(2)}) copy-start(s32[2048]{0:T(1024)S(1)} %get-tuple-element.399) | copy-start | bytes 24580
  102.3 20.3 %copy-start.27 = (s32[2048]{0:T(1024)}, s32[2048]{0:T(1024)S(1)}, u32[]{:S(2)}) copy-start(s32[2048]{0:T(1024)S(1)} %fusion.67) | copy-start | bytes 24580
  122.7 19.6 %copy-start.33 = (f32[256]{0:T(256)S(1)}, f32[256]{0:T(256)}, u32[]{:S(2)}) copy-start(f32[256]{0:T(256)} %param.24) | copy-start | bytes 3076
  122.7 19.6 %copy-start.42 = (f32[256]{0:T(256)S(1)}, f32[256]{0:T(256)}, u32[]{:S(2)}) copy-start(f32[256]{0:T(256)} %param.25) | copy-start | bytes 3076
  130.2 202.2 %copy-start.7 = (bf16[2048,256]{1,0:T(8,128)(2,1)}, bf16[2048,256]{1,0:T(8,128)(2,1)S(1)}, u32[]{:S(2)}) copy-start(bf16[2048,256]{1,0:T(8,128)(2,1)S(1)} %gather_fusion.1) | copy-start | bytes 3145732
  130.2 13.7 %copy-start.53 = (s32[1,4]{1,0:T(1,128)S(1)}, s32[1,4]{1,0:T(1,128)}, u32[]{:S(2)}) copy-start(s32[1,4]{1,0:T(1,128)} %param.23) | copy-start | bytes 52
  130.2 13.9 %copy-start.24 = (f32[256,128]{1,0:T(8,128)S(1)}, f32[256,128]{1,0:T(8,128)}, u32[]{:S(2)}) copy-start(f32[256,128]{1,0:T(8,128)} %param.28) | copy-start | bytes 393220
  130.2 14.0 %copy-start.41 = (f32[2,256]{1,0:T(2,128)S(1)}, f32[2,256]{1,0:T(2,128)}, u32[]{:S(2)}) copy-start(f32[2,256]{1,0:T(2,128)} %param.27) | copy-start | bytes 6148
  143.8 188.6 %reduce-scatter.5.cloned.1.call-start = ((), (), s32[]{:S(2)}) async-start(), calls=%async_computation.12 | async-start | bytes 10485760 | tf_op jit(solution)/shard_map/reduce_scatter | solution.py:44
  171.9 83.6 %copy-start.16 = (bf16[256,1024]{1,0:T(8,128)(2,1)}, bf16[256,1024]{1,0:T(8,128)(2,1)S(1)}, u32[]{:S(2)}) copy-start(bf16[256,1024]{1,0:T(8,128)(2,1)S(1)} %all_gather.30) | copy-start | bytes 1572868
  252.8 8.2 copy-start.10
  261.0 71.4 %copy-start.44 = (f32[256]{0:T(256)S(1)}, f32[256]{0:T(256)}, u32[]{:S(2)}) copy-start(f32[256]{0:T(256)} %param.29) | copy-start | bytes 3076
  261.0 84.9 %copy-start.35 = (f32[256]{0:T(256)S(1)}, f32[256]{0:T(256)}, u32[]{:S(2)}) copy-start(f32[256]{0:T(256)} %param.30) | copy-start | bytes 3076
  261.0 84.9 %copy-start.43 = (f32[256]{0:T(256)S(1)}, f32[256]{0:T(256)}, u32[]{:S(2)}) copy-start(f32[256]{0:T(256)} %param.31) | copy-start | bytes 3076
  261.0 152.1 %all-gather.15.cloned.1.call-start = ((), (), s32[]{:S(2)}) async-start(), calls=%async_computation.14 | async-start | bytes 2359296 | tf_op jit(solution)/shard_map/all_gather | solution.py:215
  262.8 85.9 %copy-start.18 = (f32[1024,128]{1,0:T(8,128)S(1)}, f32[1024,128]{1,0:T(8,128)}, u32[]{:S(2)}) copy-start(f32[1024,128]{1,0:T(8,128)} %param.34) | copy-start | bytes 1572868
  262.8 174.3 %all-gather.13.cloned.1.call-start = ((), (), s32[]{:S(2)}) async-start(), calls=%async_computation.13 | async-start | bytes 5242880 | tf_op jit(solution)/shard_map/all_gather | solution.py:40
  335.6 13.9 %copy-start.6 = (bf16[2048,256]{1,0:T(8,128)(2,1)S(1)}, bf16[2048,256]{1,0:T(8,128)(2,1)}, u32[]{:S(2)}) copy-start(bf16[2048,256]{1,0:T(8,128)(2,1)} %param.21) | copy-start | bytes 3145732
  335.6 13.9 %copy-start.26 = (s32[2048]{0:T(1024)S(1)}, s32[2048]{0:T(1024)}, u32[]{:S(2)}) copy-start(s32[2048]{0:T(1024)} %copy-done.25) | copy-start | bytes 24580
  348.7 141.3 %all-gather.17.cloned.1.call-start = ((), (), s32[]{:S(2)}) async-start(), calls=%async_computation.15 | async-start | bytes 2359296 | tf_op jit(solution)/shard_map/all_gather | solution.py:219
  349.5 54.6 %copy-start.28 = (s32[2048]{0:T(1024)S(1)}, s32[2048]{0:T(1024)}, u32[]{:S(2)}) copy-start(s32[2048]{0:T(1024)} %copy-done.27) | copy-start | bytes 24580
  349.5 175.2 %all-gather.21.cloned.1.call-start = ((), (), s32[]{:S(2)}) async-start(), calls=%async_computation.20 | async-start | bytes 5242880 | tf_op jit(solution)/shard_map/all_gather | solution.py:40
  413.1 111.6 %copy-start.51 = (f32[1024]{0:T(1024)S(1)}, f32[1024]{0:T(1024)}, u32[]{:S(2)}) copy-start(f32[1024]{0:T(1024)} %param.33) | copy-start | bytes 12292
  413.1 206.3 %reduce-scatter.9.cloned.1.call-start = ((), (), s32[]{:S(2)}) async-start(), calls=%async_computation.17 | async-start | bytes 10485760 | tf_op jit(solution)/shard_map/reduce_scatter | solution.py:44
  447.7 93.3 %copy-start.48 = (bf16[1024,1024]{1,0:T(8,128)(2,1)S(1)}, bf16[1024,1024]{1,0:T(8,128)(2,1)}, u32[]{:S(2)}) copy-start(bf16[1024,1024]{1,0:T(8,128)(2,1)} %all-gather.15.cloned.1.call-done) | copy-start | bytes 6291460
  548.0 145.2 %reduce-scatter.7.cloned.1.call-start = ((), (), s32[]{:S(2)}) async-start(), calls=%async_computation.16 | async-start | bytes 10485760 | tf_op jit(solution)/shard_map/reduce_scatter | solution.py:44
  563.0 56.4 %copy-start.9 = (f32[2048,256]{1,0:T(8,128)S(1)}, f32[2048,256]{1,0:T(8,128)}, u32[]{:S(2)}) copy-start(f32[2048,256]{1,0:T(8,128)} %get-tuple-element.522) | copy-start | bytes 6291460
  563.0 130.2 %copy-start.11 = (bf16[2048,256]{1,0:T(8,128)(2,1)S(1)}, bf16[2048,256]{1,0:T(8,128)(2,1)}, u32[]{:S(2)}) copy-start(bf16[2048,256]{1,0:T(8,128)(2,1)} %gather_fusion.5) | copy-start | bytes 3145732
  563.0 130.2 %copy-start.45 = (f32[256]{0:T(256)S(1)}, f32[256]{0:T(256)}, u32[]{:S(2)}) copy-start(f32[256]{0:T(256)} %param.35) | copy-start | bytes 3076
  563.0 171.8 %all-gather.19.cloned.1.call-start = ((), (), s32[]{:S(2)}) async-start(), calls=%async_computation.18 | async-start | bytes 5242880 | tf_op jit(solution)/shard_map/all_gather | solution.py:40
  699.6 388.3 %reduce-scatter.11.cloned.1.call-start = ((), (), s32[]{:S(2)}) async-start(), calls=%async_computation.19 | async-start | bytes 10485760 | tf_op jit(solution)/shard_map/reduce_scatter | solution.py:44
  758.4 4.0 copy-start.2
  767.9 21.1 %copy-start.3 = (f32[1536,4,64]{0,2,1:T(8,128)S(1)}, f32[1536,4,64]{0,2,1:T(8,128)}, u32[]{:S(2)}) copy-start(f32[1536,4,64]{0,2,1:T(8,128)} %fusion.136) | copy-start | bytes 4718596 | tf_op jit(solution)/shard_map/while
  823.9 21.1 %copy-start.3 = (f32[1536,4,64]{0,2,1:T(8,128)S(1)}, f32[1536,4,64]{0,2,1:T(8,128)}, u32[]{:S(2)}) copy-start(f32[1536,4,64]{0,2,1:T(8,128)} %fusion.136) | copy-start | bytes 4718596 | tf_op jit(solution)/shard_map/while
  870.3 4.0 copy-start.2
  879.9 21.1 %copy-start.3 = (f32[1536,4,64]{0,2,1:T(8,128)S(1)}, f32[1536,4,64]{0,2,1:T(8,128)}, u32[]{:S(2)}) copy-start(f32[1536,4,64]{0,2,1:T(8,128)} %fusion.136) | copy-start | bytes 4718596 | tf_op jit(solution)/shard_map/while
  935.7 20.5 %copy-start.3 = (f32[1536,4,64]{0,2,1:T(8,128)S(1)}, f32[1536,4,64]{0,2,1:T(8,128)}, u32[]{:S(2)}) copy-start(f32[1536,4,64]{0,2,1:T(8,128)} %fusion.136) | copy-start | bytes 4718596 | tf_op jit(solution)/shard_map/while
  967.4 4.6 copy-start.50
  978.9 14.6 %copy-start.52 = (f32[1024]{0:T(1024)S(1)}, f32[1024]{0:T(1024)}, u32[]{:S(2)}) copy-start(f32[1024]{0:T(1024)} %param.33) | copy-start | bytes 12292
  988.0 31.7 %all-to-all-start.1 = ((bf16[8,256,256]{2,1,0:T(8,128)(2,1)}), bf16[8,256,256]{2,1,0:T(8,128)(2,1)S(1)}, u32[]{:S(2)}, u32[]{:S(2)}) async-start(bf16[8,256,256]{2,1,0:T(8,128)(2,1)} %bitcast.19), calls=%async_computation.3 | async-start | bytes 2097152 | tf_op jit(solution)/shard_map/all_to_all | solution.py:322
  993.5 10.7 copy-start.15
  993.5 10.7 copy-start.47
  1019.7 63.7 %all-to-all-start.5 = ((bf16[8,1280,128]{2,1,0:T(8,128)(2,1)}), bf16[8,1280,128]{2,1,0:T(8,128)(2,1)}, u32[]{:S(2)}, u32[]{:S(2)}) async-start(bf16[8,1280,128]{2,1,0:T(8,128)(2,1)} %bitcast_bitcast_fusion), calls=%async_computation.9 | async-start | bytes 5242880 | tf_op jit(solution)/shard_map/all_to_all | solution.py:22
  1024.3 8.4 copy-start.13
  1024.4 8.4 copy-start.46
  1038.5 49.5 %copy-start.8 = (bf16[2048,256]{1,0:T(8,128)(2,1)S(1)}, bf16[2048,256]{1,0:T(8,128)(2,1)}, u32[]{:S(2)}) copy-start(bf16[2048,256]{1,0:T(8,128)(2,1)} %copy-done.7) | copy-start | bytes 3145732
  1038.5 49.5 %copy-start.21 = (f32[2048]{0:T(1024)S(1)}, f32[2048]{0:T(1024)}, u32[]{:S(2)}) copy-start(f32[2048]{0:T(1024)} %copy-done.20) | copy-start | bytes 24580
  1038.5 49.5 %copy-start.23 = (f32[2048]{0:T(1024)S(1)}, f32[2048]{0:T(1024)}, u32[]{:S(2)}) copy-start(f32[2048]{0:T(1024)} %copy-done.22) | copy-start | bytes 24580
  1038.5 49.5 %copy-start.34 = (f32[256]{0:T(256)S(1)}, f32[256]{0:T(256)}, u32[]{:S(2)}) copy-start(f32[256]{0:T(256)} %param.24) | copy-start | bytes 3076
  1083.4 85.9 %all-to-all-start.4 = ((bf16[8,128,1792]{1,2,0:T(8,128)(2,1)}), bf16[8,128,1792]{1,2,0:T(8,128)(2,1)}, u32[]{:S(2)}, u32[]{:S(2)}) async-start(bf16[8,128,1792]{1,2,0:T(8,128)(2,1)} %copy_bitcast_fusion), calls=%async_computation.8 | async-start | bytes 7340032 | tf_op jit(solution)/shard_map/all_to_all | solution.py:22
  1105.3 68.0 %copy-start.30 = (s32[2048]{0:T(1024)S(1)}, s32[2048]{0:T(1024)}, u32[]{:S(2)}) copy-start(s32[2048]{0:T(1024)} %copy-done.29) | copy-start | bytes 24580
  1169.3 65.9 %all-to-all-start.3 = ((bf16[8,256,256]{2,1,0:T(8,128)(2,1)}), bf16[8,256,256]{2,1,0:T(8,128)(2,1)S(1)}, u32[]{:S(2)}, u32[]{:S(2)}) async-start(bf16[8,256,256]{2,1,0:T(8,128)(2,1)} %bitcast.27), calls=%async_computation.7 | async-start | bytes 2097152 | tf_op jit(solution)/shard_map/all_to_all | solution.py:325
  1192.9 4.6 copy-start.36
  1192.9 4.6 copy-start.37
  1192.9 4.6 copy-start.38
  1192.9 4.6 copy-start.39
  1192.9 4.6 copy-start.40
  1235.1 9.1 copy-start.1
  (16 other events, 32.4 us)
Sparse Core Ops, SparseCore 0:
  94.0 52.8 all-gather.10
  149.0 33.1 all-gather.8
  261.1 71.2 reduce-scatter.4
  335.0 66.3 all-gather.14
  403.4 33.6 all-gather.12
  439.6 50.3 all-gather.16
  491.5 33.1 all-gather.20
  548.1 71.2 reduce-scatter.8
  621.9 71.2 reduce-scatter.6
  699.8 34.9 all-gather.18
  977.9 71.2 reduce-scatter.10
where the time goes:
time: 1260 us; the launch traced here: 1250 us
  waiting for transfers between devices  465 us (37%)
  local copies, waits for them, and re-layouts  280 us (22%)
  matrix products  204 us (16%)
  blocking collectives  154 us (12%)
  other arithmetic  100 us (8%)
  starting transfers between devices  27 us (2%)
  between operations  15.1 us (1%)
    reduce_scatter x4, waiting for transfers between devices, partial_sums(): lax.psum_scatter(partial_rows, 'narrow', scatter_dimension=1, tiled=True)  186 us
    all_gather x4, waiting for transfers between devices, feature_gather(): return lax.all_gather(share_rows, 'narrow', axis=1, tiled=True)  104 us
    all_to_all x2, waiting for transfers between devices, sent_and_summed(): parts = lax.all_to_all(split_up(shard, dim, length), axis, 0, 0, tiled=True)  99.9 us
    scatter x1, local copies, waits for them, and re-layouts, local(): jnp.zeros((total_rows,), jnp.int32).at[routing]  60.3 us
    all_to_all x1, blocking collectives, local(): lax.all_to_all(cotangent[send_index], 'wide', split_axis=0, concat_axis=0...  47 us
    dynamic_update_slice x8, local copies, waits for them, and re-layouts, attention_backward(): lax.scan(one_block, (empty_grad, empty_grad), (jnp.arange(block_count, dt...  45.7 us
    all_gather x1, waiting for transfers between devices, local(): lax.all_gather(down_low, 'wide', axis=1, tiled=True)  42.2 us
    psum x4, blocking collectives, row_totals(): return lax.psum((first, second), 'narrow')  42.2 us
  transfers between devices with their start and end apart: 16, of which 12 were waited for; matrix products, arithmetic and copies ran while one was open for 12% of the time, Pallas kernels for 0%

commit v1 on v0

v1 whole, which is shorter than its diff:
```python
import jax
import jax.numpy as jnp
from jax import lax
from jax.experimental import pallas as pl
from jax.experimental.pallas import tpu as pltpu
from jax.sharding import PartitionSpec as P

D = 1024
NORM_EPS = 1e-05

HEAD_DIM = 64
BLK = 256
NT = (((1,), (1,)), ((), ()))
NEG = -1e30


def head_mask(x, h):
    lane = lax.broadcasted_iota(jnp.int32, x.shape, 1)
    keep = (lane >= h * HEAD_DIM) & (lane < (h + 1) * HEAD_DIM)
    return jnp.where(keep, x, jnp.zeros_like(x))


def attn_fwd_kernel(first_ref, q_ref, k_ref, v_ref, start_ref, o_ref, lse_ref, s_ref, m_ref, l_ref, acc_ref):
    heads = q_ref.shape[1] // HEAD_DIM
    i = pl.program_id(0)
    lo = first_ref[i]
    q = q_ref[...] * jnp.bfloat16(HEAD_DIM ** -0.5)
    qs = [head_mask(q, h) for h in range(heads)]
    start = start_ref[...]
    q_pos = i * BLK + lax.broadcasted_iota(jnp.int32, (BLK, BLK), 0)
    k_iota = lax.broadcasted_iota(jnp.int32, (BLK, BLK), 1)
    m_ref[...] = jnp.full_like(m_ref, NEG)
    l_ref[...] = jnp.zeros_like(l_ref)
    acc_ref[...] = jnp.zeros_like(acc_ref)

    def scores(j, carry):
        rows = pl.ds(pl.multiple_of(j * BLK, BLK), BLK)
        kb = k_ref[rows, :]
        k_pos = j * BLK + k_iota
        allowed = (k_pos >= start[:, :1]) & (k_pos <= q_pos)
        for h in range(heads):
            s = lax.dot_general(qs[h], kb, NT, preferred_element_type=jnp.float32)
            s = jnp.where(allowed, s, NEG)
            s_ref[j - lo, h] = s
            m_ref[h] = jnp.maximum(m_ref[h], jnp.maximum(s[:, :128], s[:, 128:]))
        return carry

    lax.fori_loop(lo, i + 1, scores, 0)
    tops = []
    for h in range(heads):
        top = jnp.max(m_ref[h], axis=1, keepdims=True)
        tops.append(top)

    def mix(j, carry):
        rows = pl.ds(pl.multiple_of(j * BLK, BLK), BLK)
        vb = v_ref[rows, :]
        total = acc_ref[...]
        for h in range(heads):
            p = jnp.exp(s_ref[j - lo, h] - tops[h])
            l_ref[h] += p[:, :128] + p[:, 128:]
            total += jnp.dot(p.astype(jnp.bfloat16), head_mask(vb, h), preferred_element_type=jnp.float32)
        acc_ref[...] = total
        return carry

    lax.fori_loop(lo, i + 1, mix, 0)
    lane = lax.broadcasted_iota(jnp.int32, acc_ref.shape, 1)
    inv = jnp.zeros(acc_ref.shape, jnp.float32)
    column = lax.broadcasted_iota(jnp.int32, (BLK, 128), 1)
    sums = jnp.zeros((BLK, 128), jnp.float32)
    for h in range(heads):
        low = jnp.sum(l_ref[h], axis=1, keepdims=True)
        inv = jnp.where(lane // HEAD_DIM == h, 1.0 / low, inv)
        sums = jnp.where(column == h, tops[h] + jnp.log(low), sums)
    o_ref[...] = (acc_ref[...] * inv).astype(o_ref.dtype)
    lse_ref[...] = sums.T[:8]


def attention_forward(proj, first, start):
    rows = proj.shape[0]
    width = proj.shape[1] // 3
    heads = width // HEAD_DIM
    span = 1024 // BLK + 1
    return pl.pallas_call(
        attn_fwd_kernel,
        out_shape=(jax.ShapeDtypeStruct((rows, width), jnp.bfloat16), jax.ShapeDtypeStruct((8, rows), jnp.float32)),
        grid_spec=pltpu.PrefetchScalarGridSpec(
            num_scalar_prefetch=1,
            grid=(rows // BLK,),
            in_specs=[
                pl.BlockSpec((BLK, width), lambda i, f: (i, 0)),
                pl.BlockSpec((rows, width), lambda i, f: (0, 1)),
                pl.BlockSpec((rows, width), lambda i, f: (0, 2)),
                pl.BlockSpec((BLK, 128), lambda i, f: (i, 0)),
            ],
            out_specs=[
                pl.BlockSpec((BLK, width), lambda i, f: (i, 0)),
                pl.BlockSpec((8, BLK), lambda i, f: (0, i)),
            ],
            scratch_shapes=[
                pltpu.VMEM((span, heads, BLK, BLK), jnp.float32),
                pltpu.VMEM((heads, BLK, 128), jnp.float32),
                pltpu.VMEM((heads, BLK, 128), jnp.float32),
                pltpu.VMEM((BLK, width), jnp.float32),
            ],
        ),
        compiler_params=pltpu.CompilerParams(dimension_semantics=("arbitrary",), vmem_limit_bytes=40 << 20),
        cost_estimate=pl.CostEstimate(flops=16_000_000_000, bytes_accessed=8 << 20, transcendentals=0),
        name="attn_fwd",
    )(first, proj, proj, proj, start)


def attn_bwd_kernel(first_ref, q_ref, k_ref, v_ref, o_ref, do_ref, lse_ref, start_ref,
                    dq_ref, dk_ref, dv_ref, dk_acc, dv_acc, dq_acc, kt_ref):
    heads = q_ref.shape[1] // HEAD_DIM
    i = pl.program_id(0)
    lo = first_ref[i]

    @pl.when(i == 0)
    def _():
        dk_acc[...] = jnp.zeros_like(dk_acc)
        dv_acc[...] = jnp.zeros_like(dv_acc)
        kt_ref[...] = k_ref[...].T

    q = q_ref[...] * jnp.bfloat16(HEAD_DIM ** -0.5)
    do = do_ref[...]
    qs = [head_mask(q, h) for h in range(heads)]
    dos = [head_mask(do, h) for h in range(heads)]
    product = do.astype(jnp.float32) * o_ref[...].astype(jnp.float32)
    picker = (
        lax.broadcasted_iota(jnp.int32, (8, product.shape[1]), 1) // HEAD_DIM
        == lax.broadcasted_iota(jnp.int32, (8, product.shape[1]), 0)
    ).astype(jnp.float32)
    centre = lax.dot_general(picker, product, NT, preferred_element_type=jnp.float32, precision=lax.Precision.HIGHEST)
    lse = lse_ref[...]
    start = start_ref[...]
    k_iota = lax.broadcasted_iota(jnp.int32, (BLK, BLK), 0)
    q_pos = i * BLK + lax.broadcasted_iota(jnp.int32, (BLK, BLK), 1)
    dq_acc[...] = jnp.zeros_like(dq_acc)

    def pair(j, carry):
        at = pl.multiple_of(j * BLK, BLK)
        rows = pl.ds(at, BLK)
        kb = k_ref[rows, :]
        vb = v_ref[rows, :]
        k_pos = j * BLK + k_iota
        allowed = (k_pos >= start[:1, :]) & (k_pos <= q_pos)
        dk = dk_acc[rows, :]
        dv = dv_acc[rows, :]
        for h in range(heads):
            s = lax.dot_general(head_mask(kb, h), q, NT, preferred_element_type=jnp.float32)
            p = jnp.exp(jnp.where(allowed, s - lse[h:h + 1, :], NEG))
            dp = lax.dot_general(head_mask(vb, h), do, NT, preferred_element_type=jnp.float32)
            ds = (p * (dp - centre[h:h + 1, :])).astype(jnp.bfloat16)
            dv += jnp.dot(p.astype(jnp.bfloat16), dos[h], preferred_element_type=jnp.float32)
            dk += jnp.dot(ds, qs[h], preferred_element_type=jnp.float32)
            feats = slice(h * HEAD_DIM, (h + 1) * HEAD_DIM)
            dq_acc[feats, :] += jnp.dot(kt_ref[feats, rows], ds, preferred_element_type=jnp.float32)
        dk_acc[rows, :] = dk
        dv_acc[rows, :] = dv
        return carry

    lax.fori_loop(lo, i + 1, pair, 0)
    dq_ref[...] = (dq_acc[...].T * HEAD_DIM ** -0.5).astype(dq_ref.dtype)

    @pl.when(i == pl.num_programs(0) - 1)
    def _():
        dk_ref[...] = dk_acc[...].astype(dk_ref.dtype)
        dv_ref[...] = dv_acc[...].astype(dv_ref.dtype)


def attention_backward(proj, mixed, grad_mixed, lse, first, start_row):
    rows = proj.shape[0]
    width = proj.shape[1] // 3
    shape = jax.ShapeDtypeStruct((rows, width), jnp.bfloat16)
    tile = pl.BlockSpec((BLK, width), lambda i, f: (i, 0))
    whole = pl.BlockSpec((rows, width), lambda i, f: (0, 0))
    return pl.pallas_call(
        attn_bwd_kernel,
        out_shape=(shape, shape, shape),
        grid_spec=pltpu.PrefetchScalarGridSpec(
            num_scalar_prefetch=1,
            grid=(rows // BLK,),
            in_specs=[
                tile,
                pl.BlockSpec((rows, width), lambda i, f: (0, 1)),
                pl.BlockSpec((rows, width), lambda i, f: (0, 2)),
                tile,
                tile,
                pl.BlockSpec((8, BLK), lambda i, f: (0, i)),
                pl.BlockSpec((8, BLK), lambda i, f: (0, i)),
            ],
            out_specs=[tile, whole, whole],
            scratch_shapes=[
                pltpu.VMEM((rows, width), jnp.float32),
                pltpu.VMEM((rows, width), jnp.float32),
                pltpu.VMEM((width, BLK), jnp.float32),
                pltpu.VMEM((width, rows), jnp.bfloat16),
            ],
        ),
        compiler_params=pltpu.CompilerParams(dimension_semantics=("arbitrary",), vmem_limit_bytes=40 << 20),
        cost_estimate=pl.CostEstimate(flops=40_000_000_000, bytes_accessed=8 << 20, transcendentals=0),
        name="attn_bwd",
    )(first, proj, proj, proj, mixed, grad_mixed, lse, start_row)


def doc_tables(lengths_row, rows):
    ends = jnp.cumsum(lengths_row)
    starts = ends - lengths_row
    positions = jnp.arange(rows, dtype=jnp.int32)
    inside = (positions[:, None] >= starts[None, :]) & (positions[:, None] < ends[None, :])
    start = jnp.sum(jnp.where(inside, starts[None, :], 0), axis=1).astype(jnp.int32)
    first = start[::BLK] // BLK
    return start, first


def pick_kernel(index_ref, *refs):
    count = len(refs) // 2
    rows = refs[0].shape[0]
    column = index_ref[...].astype(jnp.float32).T[:, :1].astype(jnp.int32)
    source = lax.broadcasted_iota(jnp.int32, (BLK, rows), 1)
    chosen = jnp.where(source == column, 1.0, 0.0).astype(jnp.bfloat16)
    for x_ref, y_ref in zip(refs[:count], refs[count:]):
        y_ref[...] = jnp.dot(chosen, x_ref[...], preferred_element_type=jnp.float32).astype(y_ref.dtype)


def place_kernel(index_ref, *refs):
    count = len(refs) // 2
    rows = refs[0].shape[0]
    target = pl.program_id(0) * BLK + lax.broadcasted_iota(jnp.int32, (BLK, rows), 0)
    chosen = jnp.where(target == index_ref[:1, :], 1.0, 0.0).astype(jnp.bfloat16)
    for x_ref, y_ref in zip(refs[:count], refs[count:]):
        y_ref[...] = jnp.dot(chosen, x_ref[...], preferred_element_type=jnp.float32).astype(y_ref.dtype)


def permuted(kernel, name, index_rows, *arrays):
    rows = arrays[0].shape[0]
    picks = kernel is pick_kernel
    index_spec = pl.BlockSpec((8, BLK), lambda i: (0, i)) if picks else pl.BlockSpec((8, rows), lambda i: (0, 0))
    return pl.pallas_call(
        kernel,
        out_shape=[jax.ShapeDtypeStruct(a.shape, a.dtype) for a in arrays],
        grid=(rows // BLK,),
        in_specs=[index_spec] + [pl.BlockSpec(a.shape, lambda i: (0, 0)) for a in arrays],
        out_specs=[pl.BlockSpec((BLK, a.shape[1]), lambda i: (i, 0)) for a in arrays],
        compiler_params=pltpu.CompilerParams(dimension_semantics=("arbitrary",), vmem_limit_bytes=24 << 20),
        cost_estimate=pl.CostEstimate(flops=2 * rows * rows * 256 * len(arrays), bytes_accessed=4 << 20, transcendentals=0),
        name=name,
    )(index_rows, *arrays)


def pick(index_rows, *arrays):
    return permuted(pick_kernel, "pick_rows", index_rows, *arrays)


def place(index_rows, *arrays):
    return permuted(place_kernel, "place_rows", index_rows, *arrays)


def route_tables(routing, rows):
    groups = routing.shape[0] // rows
    me = lax.axis_index("wide")
    ids = routing.reshape(groups, rows)
    positions = jnp.arange(rows, dtype=jnp.int32)
    beyond = jnp.int32(rows * rows)
    keys = jnp.where(ids // rows == me, positions[None, :] * rows + ids % rows, beyond)
    send = (jnp.sort(keys, axis=1)[:, : rows // groups] % rows).reshape(rows)
    own = lax.dynamic_index_in_dim(ids, me, 0, keepdims=False)
    arrive = jnp.sort(own // rows * rows + positions) % rows
    return jnp.broadcast_to(send[None], (8, rows)), jnp.broadcast_to(arrive[None], (8, rows))


def exchanged(rows_out):
    return lax.all_to_all(rows_out, "wide", split_axis=0, concat_axis=0, tiled=True)


def row_stats(rows_full):
    mean = jnp.mean(rows_full, axis=1, keepdims=True)
    scale = lax.rsqrt(jnp.mean(rows_full * rows_full, axis=1, keepdims=True) - mean * mean + NORM_EPS)
    return mean, scale


def local(
    inputs,
    cotangent,
    routing,
    lengths,
    ln1_gain,
    ln1_bias,
    qkv_weight,
    qv_bias,
    out_weight,
    out_bias,
    ln2_gain,
    ln2_bias,
    up_weight,
    up_bias,
    down_weight,
    down_bias,
):
    low, wide_type = jnp.bfloat16, jnp.float32
    row_count, quarter = inputs.shape
    parts = lax.axis_size("narrow")
    share = row_count // parts
    part = lax.axis_index("narrow")
    send_rows, arrive_rows = route_tables(routing, row_count)

    def mine(rows_full):
        return lax.dynamic_slice_in_dim(rows_full, part * share, share, 0)

    def my_features(rows_full):
        return lax.dynamic_slice_in_dim(rows_full, part * quarter, quarter, 1)

    (sent,) = pick(send_rows, inputs)
    (routed,) = place(arrive_rows, exchanged(sent))
    (sent_grad,) = pick(send_rows, cotangent)
    (routed_grad,) = place(arrive_rows, exchanged(sent_grad))
    vectors = jnp.stack([ln1_gain, ln1_bias, ln2_gain, ln2_bias, out_bias, down_bias])
    vectors = lax.all_gather(vectors, "narrow", axis=1, tiled=True)
    start, first = doc_tables(lengths[0], row_count)

    qkv_full = lax.all_gather(qkv_weight.astype(low).reshape(qkv_weight.shape[0], 3 * quarter), "wide", axis=0, tiled=True)
    out_full = lax.all_gather(out_weight.astype(low), "wide", axis=1, tiled=True)
    up_full = lax.all_gather(up_weight.astype(low), "wide", axis=0, tiled=True)
    down_full = lax.all_gather(down_weight.astype(low), "wide", axis=1, tiled=True)

    routed_full = lax.all_gather(routed, "narrow", axis=1, tiled=True).astype(wide_type)
    mean_one, scale_one = row_stats(routed_full)
    act_one = ((routed_full - mean_one) * scale_one * vectors[0] + vectors[1]).astype(low)
    shift = jnp.concatenate([qv_bias[0], jnp.zeros((quarter,), wide_type), qv_bias[1]])
    proj = (jnp.dot(act_one, qkv_full, preferred_element_type=wide_type) + shift).astype(low)
    mixed, log_sums = attention_forward(proj, first, jnp.broadcast_to(start[:, None], (row_count, 128)))
    branch = jnp.dot(mixed, out_full, preferred_element_type=wide_type).astype(low)
    branch = lax.psum_scatter(branch, "narrow", scatter_dimension=0, tiled=True).astype(wide_type)
    middle = mine(routed_full) + branch + vectors[4]
    mean_two, scale_two = row_stats(middle)
    normed_two = (middle - mean_two) * scale_two
    act_two = lax.all_gather((normed_two * vectors[2] + vectors[3]).astype(low), "narrow", axis=0, tiled=True)

    grad_full = lax.all_gather(routed_grad, "narrow", axis=1, tiled=True)
    preact = jnp.dot(act_two, up_full, preferred_element_type=wide_type) + up_bias
    gelu, gelu_back = jax.vjp(lambda u: jax.nn.gelu(u, approximate=True), preact)
    hidden = gelu.astype(low)
    grad_hidden = jnp.einsum("td,fd->tf", grad_full, down_full, preferred_element_type=wide_type)
    grad_pre = gelu_back(grad_hidden)[0].astype(low)
    grad_act_two = jnp.einsum("tf,df->td", grad_pre, up_full, preferred_element_type=wide_type).astype(low)
    grad_act_two = lax.psum_scatter(grad_act_two, "narrow", scatter_dimension=0, tiled=True).astype(wide_type)
    scaled = grad_act_two * vectors[2]
    back_two = scale_two * (
        scaled
        - jnp.mean(scaled, axis=1, keepdims=True)
        - normed_two * jnp.mean(scaled * normed_two, axis=1, keepdims=True)
    )
    grad_branch = (mine(grad_full).astype(wide_type) + back_two).astype(low)
    branch_full = lax.all_gather(grad_branch, "narrow", axis=0, tiled=True)
    gain_two_grad = jnp.sum(grad_act_two * normed_two, axis=0)
    bias_two_grad = jnp.sum(grad_act_two, axis=0)

    held = jnp.arange(parts, dtype=jnp.int32)[:, None, None] == part
    kept = jnp.where(held, (middle + vectors[5])[None], 0.0).reshape(row_count, D)
    result = (jnp.dot(hidden, down_full, preferred_element_type=wide_type) + kept).astype(low)
    result = lax.psum_scatter(result, "narrow", scatter_dimension=1, tiled=True)
    down_grad = jnp.einsum("tf,td->fd", hidden, grad_full, preferred_element_type=wide_type).astype(low)
    up_grad = jnp.einsum("td,tf->df", act_two, grad_pre, preferred_element_type=wide_type).astype(low)
    down_grad = lax.psum_scatter(down_grad, "wide", scatter_dimension=1, tiled=True).astype(wide_type)
    up_grad = lax.psum_scatter(up_grad, "wide", scatter_dimension=0, tiled=True).astype(wide_type)

    out_grad = jnp.einsum("tf,td->fd", mixed, branch_full, preferred_element_type=wide_type).astype(low)
    out_grad = lax.psum_scatter(out_grad, "wide", scatter_dimension=1, tiled=True).astype(wide_type)
    grad_mixed = jnp.einsum("td,fd->tf", branch_full, out_full, preferred_element_type=wide_type).astype(low)
    grad_q, grad_k, grad_v = attention_backward(
        proj, mixed, grad_mixed, log_sums, first, jnp.broadcast_to(start[None], (8, row_count))
    )
    grad_proj = jnp.concatenate([grad_q, grad_k, grad_v], axis=1)
    grad_act_one = jnp.einsum("tc,dc->td", grad_proj, qkv_full, preferred_element_type=wide_type).astype(low)
    grad_act_one = lax.psum_scatter(grad_act_one, "narrow", scatter_dimension=1, tiled=True).astype(wide_type)
    qkv_grad = jnp.einsum("td,tc->dc", act_one, grad_proj, preferred_element_type=wide_type).astype(low)
    qkv_grad = lax.psum_scatter(qkv_grad, "wide", scatter_dimension=0, tiled=True).astype(wide_type)

    normed_one = (routed.astype(wide_type) - mean_one) * scale_one
    scaled = grad_act_one * ln1_gain
    totals = lax.psum(jnp.stack([jnp.sum(scaled, axis=1), jnp.sum(scaled * normed_one, axis=1)]), "narrow") / D
    back_one = scale_one * (scaled - totals[0][:, None] - normed_one * totals[1][:, None])
    grad_input = (my_features(branch_full).astype(wide_type) + back_one).astype(low)

    (result_sent,) = pick(arrive_rows, result)
    (outputs,) = place(send_rows, exchanged(result_sent))
    (input_sent,) = pick(arrive_rows, grad_input)
    (input_grad,) = place(send_rows, exchanged(input_sent))

    norm_two = lax.psum(jnp.stack([gain_two_grad, bias_two_grad]), ("wide", "narrow"))
    norm_two = lax.dynamic_slice_in_dim(norm_two, part * quarter, quarter, 1)
    middle_sums = lax.psum(
        (
            jnp.sum(my_features(branch_full), axis=0, dtype=wide_type),
            jnp.sum(grad_pre, axis=0, dtype=wide_type),
            jnp.sum(routed_grad, axis=0, dtype=wide_type),
        ),
        "wide",
    )
    last_sums = lax.psum(
        (
            jnp.sum(grad_act_one * normed_one, axis=0),
            jnp.sum(grad_act_one, axis=0),
            jnp.stack([jnp.sum(grad_q, axis=0, dtype=wide_type), jnp.sum(grad_v, axis=0, dtype=wide_type)]),
        ),
        "wide",
    )
    return (
        outputs,
        input_grad,
        last_sums[0],
        last_sums[1],
        qkv_grad.reshape(qkv_weight.shape),
        last_sums[2],
        out_grad,
        middle_sums[0],
        norm_two[0],
        norm_two[1],
        up_grad,
        middle_sums[1],
        down_grad,
        middle_sums[2],
    )


def solution(mesh):
    row_mat, col_mat, vector = P("wide", "narrow"), P("narrow", "wide"), P("narrow")
    projections, pair = P("wide", None, "narrow"), P(None, "narrow")
    return jax.shard_map(
        local,
        mesh=mesh,
        in_specs=(
            row_mat,
            row_mat,
            P(),
            P("wide", None),
            vector,
            vector,
            projections,
            pair,
            col_mat,
            vector,
            vector,
            vector,
            row_mat,
            vector,
            col_mat,
            vector,
        ),
        out_specs=(
            row_mat,
            row_mat,
            vector,
            vector,
            projections,
            pair,
            col_mat,
            vector,
            vector,
            vector,
            row_mat,
            vector,
            col_mat,
            vector,
        ),
        check_vma=False,
    )
```

time: 1260 us -> 966 us (0.77)
  local copies, waits for them, and re-layouts: 280 us -> 32.8 us
  matrix products: 204 us -> 95.6 us
  Pallas kernels: 0 us -> 89.6 us
  other arithmetic: 100 us -> 42 us
  waiting for transfers between devices: 465 us -> 492 us
  blocking collectives: 154 us -> 167 us
    dynamic_update_slice x16 -> x0, local copies, waits for them, and re-layouts: 122 us -> none  [the longest x8 45.7 us: attention_backward(): lax.scan(one_block, (empty_grad, empty_grad), (jnp.arange(block_count, dt...]
    dot_general x40 -> x12, matrix products: 204 us -> 95.6 us  [the longest x1 13.7 us: local(): jnp.einsum('td,fd->tf', grad_full, down_full, preferred_element_type=wide...]
    all_to_all x5 -> x3, waiting for transfers between devices: 132 us -> 38.6 us  [exchanged(): lax.all_to_all(rows_out, 'wide', split_axis=0, concat_axis=0, tiled=True)]
    pallas_call x0 -> x10, Pallas kernels: none -> 89.6 us  [the longest x8 43.2 us: permuted(): pl.pallas_call(kernel, out_shape=[jax.ShapeDtypeStruct(a.shape, a.dtype)...]
    gather x8 -> x0, local copies, waits for them, and re-layouts: 69.2 us -> none  [the longest x1 9.06 us: local(): inputs[send_index]]
    unnamed x11 -> x17, waiting for transfers between devices: 0.18 us -> 61.9 us
    scatter x1 -> x0, local copies, waits for them, and re-layouts: 60.3 us -> none  [local(): jnp.zeros((total_rows,), jnp.int32).at[routing]]
    all_gather x7, waiting for transfers between devices: 146 us -> 177 us  [the longest x1 43.2 us: local(): lax.all_gather(qkv_weight.astype(low).reshape(qkv_weight.shape[0], 3 * qu...]
  transfers between devices with their start and end apart: 16 -> 18, of which waited for: 12 -> 13; matrix products, arithmetic and copies ran while one was open for 12% -> 12% of each run, Pallas kernels for 0% -> 6%
where the time goes in v1:
time: 966 us; the launch traced here: 956 us
  waiting for transfers between devices  492 us (51%)
  blocking collectives  167 us (17%)
  matrix products  95.6 us (10%)
  Pallas kernels  89.6 us (9%)
  other arithmetic  42 us (4%)
  local copies, waits for them, and re-layouts  32.8 us (3%)
  starting transfers between devices  22.4 us (2%)
  between operations  15.1 us (2%)
    reduce_scatter x1, waiting for transfers between devices, local(): lax.psum_scatter(up_grad, 'wide', scatter_dimension=0, tiled=True)  67.2 us
    reduce_scatter x1, waiting for transfers between devices, local(): lax.psum_scatter(qkv_grad, 'wide', scatter_dimension=0, tiled=True)  66.4 us
    unnamed x17, waiting for transfers between devices  61.9 us
    all_to_all x1, blocking collectives, exchanged(): lax.all_to_all(rows_out, 'wide', split_axis=0, concat_axis=0, tiled=True)  48.8 us
    reduce_scatter x1, waiting for transfers between devices, local(): lax.psum_scatter(grad_act_two, 'narrow', scatter_dimension=0, tiled=True)  44.5 us
    pallas_call x8, Pallas kernels, permuted(): pl.pallas_call(kernel, out_shape=[jax.ShapeDtypeStruct(a.shape, a.dtype)...  43.2 us
    all_gather x1, waiting for transfers between devices, local(): lax.all_gather(qkv_weight.astype(low).reshape(qkv_weight.shape[0], 3 * qu...  43.2 us
    all_gather x1, waiting for transfers between devices, local(): lax.all_gather(down_weight.astype(low), 'wide', axis=1, tiled=True)  42.4 us
  transfers between devices with their start and end apart: 18, of which 13 were waited for; matrix products, arithmetic and copies ran while one was open for 12% of the time, Pallas kernels for 6%

profile of v1, /device:TPU:0, one launch (start us, length us, event | category | flops | bytes accessed | tf_op | source)
XLA Modules:
  0.0 956.2 jit_solution(5813722067128094315)
XLA Ops:
  8.8 8.5 sort.26.cloned.1.call-done
  19.3 6.2 pick_rows.4
  25.5 7.3 all-to-all-start
  32.9 5.0 sort.24
  37.9 20.6 %all-to-all-done = bf16[8,256,256]{2,1,0:T(8,128)(2,1)S(1)} async-done(((bf16[8,256,256]{2,1,0:T(8,128)(2,1)}), bf16[8,256,256]{2,1,0:T(8,128)(2,1)S(1)}, u32[]{:S(2)}, u32[]{:S(2)}) %all-to-all-start) | async-done | bytes 1048608 | tf_op jit(solution)/shard_map/all_to_all | solution.py:273
  58.7 4.8 place_rows.4
  65.0 5.2 all_gather.28
  70.3 27.7 %all_gather.30 = bf16[256,1024]{1,0:T(8,128)(2,1)S(1)} all-gather(bf16[256,128]{1,0:T(8,128)(2,1)S(1)} %convert_element_type.108), channel_id=1, replica_groups=mesh['wide'=8,'narrow'=4] {'wide'}, dimensions={1}, use_global_device_ids=true | all-gather | bytes 589824 | tf_op jit(solution)/shard_map/all_gather | solution.py:322
  97.9 3.6 convert_reduce_fusion.1
  101.6 43.2 %all-gather.10.cloned.1.call-done = bf16[1024,768]{0,1:T(8,128)(2,1)} async-done(((bf16[128,768]{0,1:T(8,128)(2,1)}), bf16[1024,768]{0,1:T(8,128)(2,1)}) %all-gather.10.cloned.1.call-update) | async-done | bytes 1572880 | tf_op jit(solution)/shard_map/all_gather | solution.py:321
  144.8 6.9 add_convert_fusion.1.q_ref.k_ref.v_ref
  152.1 17.8 %attn_fwd.1 = (bf16[2048,256]{1,0:T(8,128)(2,1)S(1)}, f32[8,2048]{1,0:T(8,128)S(1)}) custom-call(s32[8]{0:T(128)S(1)} %and_select_fusion.first_ref, bf16[2048,768]{1,0:T(8,128)(2,1)S(1)} %add_convert_fusion.1.q_ref.k_ref.v_ref, bf16[2048,768]{1,0:T(8,128)(2,1)S(1)} %add_convert_fusion.1.q_ref.k_ref.v_ref, ...), custom_call_target="tpu_custom_call" | custom-call | flops 16000000000 | bytes 8388608 | tf_op jit(solution)/shard_map/attn_fwd/pallas_call | solution.py:83
  169.9 3.2 convolution_convert_fusion
  175.4 7.5 convert_element_type.104
  182.9 36.0 %reduce-scatter.13.cloned.1.call-done = bf16[512,1024]{1,0:T(8,128)(2,1)} async-done(((bf16[2048,1024]{1,0:T(8,128)(2,1)}), bf16[512,1024]{1,0:T(8,128)(2,1)}) %reduce-scatter.13.cloned.1.call-update) | async-done | bytes 1048592 | tf_op jit(solution)/shard_map/reduce_scatter | solution.py:333
  218.8 2.5 fusion.40
  221.4 1.3 copy-done.7
  222.7 1.4 add_convert_fusion.2
  225.0 5.6 pick_rows.6
  230.6 48.8 %all_to_all.44 = bf16[8,256,256]{2,1,0:T(8,128)(2,1)S(1)} all-to-all(bf16[8,256,256]{2,1,0:T(8,128)(2,1)S(1)} %bitcast.84), channel_id=1, replica_groups=mesh['wide'=8,'narrow'=4] {'wide'}, dimensions={0} | all-to-all | bytes 2097152 | tf_op jit(solution)/shard_map/all_to_all | solution.py:273
  279.3 4.8 place_rows.6
  284.3 33.1 %all-gather.12.cloned.1.call-done = bf16[2048,1024]{1,0:T(8,128)(2,1)} async-done(((bf16[512,1024]{1,0:T(8,128)(2,1)}), bf16[2048,1024]{1,0:T(8,128)(2,1)}) %all-gather.12.cloned.1.call-update) | async-done | bytes 4194320 | tf_op jit(solution)/shard_map/all_gather | solution.py:337
  317.4 10.6 %fusion.46 = f32[2048,1024]{1,0:T(8,128)} fusion(bf16[2048,1024]{1,0:T(8,128)(2,1)} %all-gather.12.cloned.1.call-done, bf16[1024,1024]{1,0:T(8,128)(2,1)} %all-gather.14.cloned.1.call-done), kind=kOutput, calls=%fused_computation.123 | convolution fusion | flops 4294967296 | bytes 14680064 | tf_op jit(solution)/shard_map/dot_general | solution.py:340
  328.0 42.4 %all-gather.16.cloned.1.call-done = bf16[1024,1024]{1,0:T(8,128)(2,1)} async-done(((bf16[1024,128]{1,0:T(8,128)(2,1)}), bf16[1024,1024]{1,0:T(8,128)(2,1)}) %all-gather.16.cloned.1.call-update) | async-done | bytes 2097168 | tf_op jit(solution)/shard_map/all_gather | solution.py:324
  370.4 34.8 %all-gather.18.cloned.1.call-done = bf16[2048,1024]{1,0:T(8,128)(2,1)} async-done(((bf16[2048,256]{1,0:T(8,128)(2,1)}), bf16[2048,1024]{1,0:T(8,128)(2,1)}) %all-gather.18.cloned.1.call-update) | async-done | bytes 4194320 | tf_op jit(solution)/shard_map/all_gather | solution.py:339
  405.2 13.7 %convert_reduce_fusion = (f32[1024]{0:T(1024)S(1)}, bf16[2048,1024]{1,0:T(8,128)(2,1)S(1)}) fusion(f32[2048,1024]{1,0:T(8,128)} %fusion.46, f32[1024]{0:T(1024)S(1)} %copy-done.22, bf16[2048,1024]{1,0:T(8,128)(2,1)} %all-gather.18.cloned.1.call-done, bf16[1024,1024]{1,0:T(8,128)(2,1)} %all-gather.16.cloned.1.call-done), kind=kOutput, calls=%fused_computation.12 | convolution fusion | flops 4343200768 | bytes 18882560 | tf_op jit(solution)/shard_map/td,fd->tf/dot_general | solution.py:343
  418.8 2.0 copy-done.36
  420.8 6.3 convolution_convert_fusion.2
  427.3 44.5 %reduce-scatter.17.cloned.1.call-done = bf16[512,1024]{1,0:T(8,128)(2,1)} async-done(((bf16[2048,1024]{1,0:T(8,128)(2,1)}), bf16[512,1024]{1,0:T(8,128)(2,1)}) %reduce-scatter.17.cloned.1.call-update) | async-done | bytes 1048592 | tf_op jit(solution)/shard_map/reduce_scatter | solution.py:346
  471.8 2.2 fusion.24
  474.0 4.0 fusion.22
  478.3 10.7 %fusion.8 = bf16[2048,1024]{1,0:T(8,128)(2,1)} fusion(f32[512,1024]{1,0:T(8,128)} %get-tuple-element.107, pred[2048]{0:T(1024)(128)(4,1)S(1)} %bitcast.106, bf16[1024,1024]{1,0:T(8,128)(2,1)} %all-gather.16.cloned.1.call-done, f32[2048,1024]{1,0:T(8,128)} %fusion.46, f32[1024]{0:T(1024)S(1)} %copy-done.22), kind=kOutput, calls=%fused_computation.11 | convolution fusion | flops 4322230272 | bytes 16783360 | tf_op jit(solution)/shard_map/dot_general | solution.py:360
  489.0 23.7 %all-gather.20.cloned.1.call-done = bf16[2048,1024]{1,0:T(8,128)(2,1)} async-done(((bf16[512,1024]{1,0:T(8,128)(2,1)}), bf16[2048,1024]{1,0:T(8,128)(2,1)}) %all-gather.20.cloned.1.call-update) | async-done | bytes 4194320 | tf_op jit(solution)/shard_map/all_gather | solution.py:354
  512.7 3.6 convolution_convert_fusion.3.do_ref
  516.4 28.5 %attn_bwd.1 = (bf16[2048,256]{1,0:T(8,128)(2,1)S(1)}, bf16[2048,256]{1,0:T(8,128)(2,1)S(1)}, bf16[2048,256]{1,0:T(8,128)(2,1)S(1)}) custom-call(s32[8]{0:T(128)S(1)} %and_select_fusion.first_ref, bf16[2048,768]{1,0:T(8,128)(2,1)S(1)} %copy-done.6, bf16[2048,768]{1,0:T(8,128)(2,1)S(1)} %copy-done.6, bf16[2048,768]{1,0:T(8,128)(2,1)S(1)} %copy-done.6, ...), custom_call_target="tpu_custom_call" | custom-call | flops 40000000000 | bytes 8388608 | tf_op jit(solution)/shard_map/attn_bwd/pallas_call | solution.py:177
  545.2 1.6 copy-done.14
  546.9 4.9 convolution_convert_fusion.1
  552.1 12.0 %convolution_convert_fusion.4 = bf16[1024,1024]{1,0:T(8,128)(2,1)} fusion(bf16[2048,1024]{1,0:T(8,128)(2,1)} %all-gather.18.cloned.1.call-done, f32[2048,1024]{1,0:T(8,128)} %fusion.46, f32[1024]{0:T(1024)S(1)} %copy-done.22), kind=kOutput, calls=%fused_computation.55 | convolution fusion | flops 4316987392 | bytes 14684160 | tf_op jit(solution)/shard_map/tf,td->fd/dot_general | solution.py:362
  564.1 3.9 copy.42
  568.1 10.6 %convolution_convert_fusion.5 = bf16[1024,1024]{1,0:T(8,128)(2,1)} fusion(bf16[2048,1024]{1,0:T(8,128)(2,1)} %all-gather.12.cloned.1.call-done, bf16[2048,1024]{1,0:T(8,128)(2,1)} %copy-done.36), kind=kOutput, calls=%fused_computation.56 | convolution fusion | flops 4296015872 | bytes 10485760 | tf_op jit(solution)/shard_map/td,tf->df/dot_general | solution.py:363
  578.8 4.8 convolution_convert_fusion.7
  583.6 2.0 copy.40
  586.0 8.3 convolution_convert_fusion.6
  594.4 1.2 copy-done.4
  595.6 5.5 pick_rows.5
  602.1 9.1 all-to-all-start.1
  611.2 2.6 fusion.25
  613.8 10.9 %psum.56 = f32[2,2048]{1,0:T(2,128)S(1)} all-reduce(f32[2,2048]{1,0:T(2,128)S(1)} %pad_maximum_fusion), channel_id=1, replica_groups=mesh['wide'=8,'narrow'=4] {'narrow'}, use_global_device_ids=true, to_apply=%region_16.17 | all-reduce | flops 4096 | bytes 32768 | tf_op jit(solution)/shard_map/psum | solution.py:381
  624.7 3.5 convert_reduce_fusion.4
  628.2 5.5 pick_rows.7
  634.7 18.0 %all-to-all-done.1 = bf16[8,256,256]{2,1,0:T(8,128)(2,1)S(1)} async-done(((bf16[8,256,256]{2,1,0:T(8,128)(2,1)}), bf16[8,256,256]{2,1,0:T(8,128)(2,1)S(1)}, u32[]{:S(2)}, u32[]{:S(2)}) %all-to-all-start.1) | async-done | bytes 1048608 | tf_op jit(solution)/shard_map/all_to_all | solution.py:273
  652.7 4.2 all-to-all-start.3
  656.9 1.5 convert_reduce_fusion.5
  658.4 39.4 %reduce-scatter.27.cloned.1.call-done = bf16[128,1024]{1,0:T(8,128)(2,1)} async-done(((bf16[1024,1024]{1,0:T(8,128)(2,1)}), bf16[128,1024]{1,0:T(8,128)(2,1)}) %reduce-scatter.27.cloned.1.call-update) | async-done | bytes 262160
  697.9 1.8 copy.43
  699.7 1.8 convert_element_type.136
  701.4 67.2 %reduce-scatter.23.cloned.1.call-done = bf16[128,1024]{1,0:T(8,128)(2,1)} async-done(((bf16[1024,1024]{1,0:T(8,128)(2,1)}), bf16[128,1024]{1,0:T(8,128)(2,1)}) %reduce-scatter.23.cloned.1.call-update) | async-done | bytes 262160 | tf_op jit(solution)/shard_map/reduce_scatter | solution.py:365
  768.6 1.8 convert_element_type.133
  770.5 39.7 %psum.61 = f32[2,1024]{1,0:T(2,128)S(1)} all-reduce(f32[2,1024]{1,0:T(2,128)S(1)} %pad_maximum_fusion.1), channel_id=1, replica_groups=mesh['wide'=8,'narrow'=4] {'wide','narrow'}, use_global_device_ids=true, to_apply=%region_30.31 | all-reduce | flops 2048 | bytes 16384 | tf_op jit(solution)/shard_map/psum | solution.py:390
  811.4 22.2 %reduce-scatter.25.cloned.1.call-done = bf16[128,256]{1,0:T(8,128)(2,1)} async-done(((bf16[1024,256]{1,0:T(8,128)(2,1)}), bf16[128,256]{1,0:T(8,128)(2,1)}) %reduce-scatter.25.cloned.1.call-update) | async-done | bytes 65552
  835.2 66.4 %reduce-scatter.21.cloned.1.call-done = bf16[128,768]{1,0:T(8,128)(2,1)} async-done(((bf16[1024,768]{1,0:T(8,128)(2,1)}), bf16[128,768]{1,0:T(8,128)(2,1)}) %reduce-scatter.21.cloned.1.call-update) | async-done | bytes 196624 | tf_op jit(solution)/shard_map/reduce_scatter | solution.py:377
  903.6 4.8 place_rows.5
  908.5 34.7 %all-reduce = (f32[256]{0:T(256)}, f32[256]{0:T(256)}, f32[2,256]{1,0:T(2,128)}, f32[256]{0:T(256)}, f32[1024]{0:T(1024)}, /*index=5*/f32[256]{0:T(256)}) all-reduce(f32[256]{0:T(256)S(1)} %get-tuple-element.87, f32[256]{0:T(256)S(1)} %get-tuple-element.94, ...), channel_id=1, replica_groups=mesh['wide'=8,'narrow'=4] {'wide'}, use_global_device_ids=true, to_apply=%region_18.19 | all-reduce | flops 2560 | bytes 20480 | tf_op jit(solution)/shard_map/psum | solution.py:400
  943.2 6.1 place_rows.7
  (155 shorter events, 17.0 us)
Async XLA Ops:
  7.2 10.2 %sort.26.cloned.1.call-start = ((), (), s32[]{:S(2)}) async-start(), calls=%async_computation.27 | async-start | bytes 196640 | tf_op jit(solution)/shard_map/jit(sort)/sort | solution.py:266
  18.1 1.2 copy-start.2
  25.5 33.1 %all-to-all-start = ((bf16[8,256,256]{2,1,0:T(8,128)(2,1)}), bf16[8,256,256]{2,1,0:T(8,128)(2,1)S(1)}, u32[]{:S(2)}, u32[]{:S(2)}) async-start(bf16[8,256,256]{2,1,0:T(8,128)(2,1)} %bitcast.1), calls=%async_computation | async-start | bytes 2097152 | tf_op jit(solution)/shard_map/all_to_all | solution.py:273
  32.8 65.1 %all-gather.8.cloned.1.call-start = ((), (), s32[]{:S(2)}) async-start(), calls=%async_computation.12 | async-start | bytes 5242880 | tf_op jit(solution)/shard_map/all_gather | solution.py:326
  58.6 5.0 copy-start.13
  58.6 5.9 copy-start.35
  58.6 6.3 copy-start.15
  58.6 6.3 copy-start.20
  58.6 6.3 copy-start.28
  58.6 6.3 copy-start.29
  58.6 6.3 copy-start.30
  58.6 6.3 copy-start.31
  58.7 6.3 copy-start.32
  58.7 11.5 %copy-start.27 = (f32[2,256]{1,0:T(2,128)S(1)}, f32[2,256]{1,0:T(2,128)}, u32[]{:S(2)}) copy-start(f32[2,256]{1,0:T(2,128)} %param.23) | copy-start | bytes 6148
  63.6 81.2 %all-gather.10.cloned.1.call-start = ((), (), s32[]{:S(2)}) async-start(), calls=%async_computation.13 | async-start | bytes 1769472 | tf_op jit(solution)/shard_map/all_gather | solution.py:321
  64.5 154.4 %reduce-scatter.13.cloned.1.call-start = ((), (), s32[]{:S(2)}) async-start(), calls=%async_computation.14 | async-start | bytes 5242880 | tf_op jit(solution)/shard_map/reduce_scatter | solution.py:333
  70.3 81.4 %copy-start.23 = (f32[1,1024]{1,0:T(1,128)}, f32[1,1024]{1,0:T(1,128)S(1)}, u32[]{:S(2)}) copy-start(f32[1,1024]{1,0:T(1,128)S(1)} %get-tuple-element.112) | copy-start | bytes 12292
  70.3 81.4 %copy-start.25 = (f32[1,1024]{1,0:T(1,128)}, f32[1,1024]{1,0:T(1,128)S(1)}, u32[]{:S(2)}) copy-start(f32[1,1024]{1,0:T(1,128)S(1)} %get-tuple-element.113) | copy-start | bytes 12292
  97.9 71.9 %copy-start.9 = (bf16[256,1024]{1,0:T(8,128)(2,1)}, bf16[256,1024]{1,0:T(8,128)(2,1)S(1)}, u32[]{:S(2)}) copy-start(bf16[256,1024]{1,0:T(8,128)(2,1)S(1)} %all_gather.30) | copy-start | bytes 1572868
  101.6 50.1 %copy-start.16 = (f32[2048]{0:T(1024)}, f32[2048]{0:T(1024)S(1)}, u32[]{:S(2)}) copy-start(f32[2048]{0:T(1024)S(1)} %get-tuple-element.118) | copy-start | bytes 24580
  101.6 50.1 %copy-start.18 = (f32[2048]{0:T(1024)}, f32[2048]{0:T(1024)S(1)}, u32[]{:S(2)}) copy-start(f32[2048]{0:T(1024)S(1)} %get-tuple-element.119) | copy-start | bytes 24580
  151.7 18.1 %copy-start.5 = (bf16[2048,768]{1,0:T(8,128)(2,1)}, bf16[2048,768]{1,0:T(8,128)(2,1)S(1)}, u32[]{:S(2)}) copy-start(bf16[2048,768]{1,0:T(8,128)(2,1)S(1)} %add_convert_fusion.1.q_ref.k_ref.v_ref) | copy-start | bytes 9437188
  173.1 1.0 copy-start.11
  173.1 111.2 %all-gather.14.cloned.1.call-start = ((), (), s32[]{:S(2)}) async-start(), calls=%async_computation.16 | async-start | bytes 2359296 | tf_op jit(solution)/shard_map/all_gather | solution.py:323
  174.9 142.5 %all-gather.12.cloned.1.call-start = ((), (), s32[]{:S(2)}) async-start(), calls=%async_computation.15 | async-start | bytes 5242880 | tf_op jit(solution)/shard_map/all_gather | solution.py:337
  218.8 5.3 copy-start.12
  218.8 6.1 copy-start.3
  221.4 1.4 copy-start.7
  224.1 146.3 %all-gather.16.cloned.1.call-start = ((), (), s32[]{:S(2)}) async-start(), calls=%async_computation.17 | async-start | bytes 2359296 | tf_op jit(solution)/shard_map/all_gather | solution.py:324
  224.9 180.2 %all-gather.18.cloned.1.call-start = ((), (), s32[]{:S(2)}) async-start(), calls=%async_computation.19 | async-start | bytes 5242880 | tf_op jit(solution)/shard_map/all_gather | solution.py:339
  284.2 121.0 %copy-start.22 = (f32[1024]{0:T(1024)S(1)}, f32[1024]{0:T(1024)}, u32[]{:S(2)}) copy-start(f32[1024]{0:T(1024)} %param.29) | copy-start | bytes 12292
  284.2 187.7 %reduce-scatter.17.cloned.1.call-start = ((), (), s32[]{:S(2)}) async-start(), calls=%async_computation.20 | async-start | bytes 5242880 | tf_op jit(solution)/shard_map/reduce_scatter | solution.py:346
  328.0 92.8 %copy-start.33 = (bf16[1024,1024]{1,0:T(8,128)(2,1)S(1)}, bf16[1024,1024]{1,0:T(8,128)(2,1)}, u32[]{:S(2)}) copy-start(bf16[1024,1024]{1,0:T(8,128)(2,1)} %all-gather.14.cloned.1.call-done) | copy-start | bytes 6291460
  418.8 2.0 copy-start.36
  427.1 44.8 %copy-start.8 = (f32[512,1024]{1,0:T(8,128)S(1)}, f32[512,1024]{1,0:T(8,128)}, u32[]{:S(2)}) copy-start(f32[512,1024]{1,0:T(8,128)} %copy-done.7) | copy-start | bytes 6291460
  427.1 85.6 %all-gather.20.cloned.1.call-start = ((), (), s32[]{:S(2)}) async-start(), calls=%async_computation.21 | async-start | bytes 5242880 | tf_op jit(solution)/shard_map/all_gather | solution.py:354
  478.1 116.2 %reduce-scatter.15.cloned.1.call-start = ((), (), s32[]{:S(2)}) async-start(), calls=%async_computation.18 | async-start | bytes 5242880 | tf_op jit(solution)/shard_map/reduce_scatter | solution.py:361
  488.9 23.8 %copy-start.10 = (bf16[256,1024]{1,0:T(8,128)(2,1)S(1)}, bf16[256,1024]{1,0:T(8,128)(2,1)}, u32[]{:S(2)}) copy-start(bf16[256,1024]{1,0:T(8,128)(2,1)} %copy-done.9) | copy-start | bytes 1572868
  489.0 122.2 %reduce-scatter.19.cloned.1.call-start = ((), (), s32[]{:S(2)}) async-start(), calls=%async_computation.22 | async-start | bytes 5242880 | tf_op jit(solution)/shard_map/reduce_scatter | solution.py:375
  512.7 3.7 copy-start.6
  545.0 1.9 copy-start.34
  545.2 1.6 copy-start.14
  551.8 146.1 %reduce-scatter.27.cloned.1.call-start = ((), (), s32[]{:S(2)}) async-start(), calls=%async_computation.26 | async-start | bytes 2359296
  568.0 200.6 %reduce-scatter.23.cloned.1.call-start = ((), (), s32[]{:S(2)}) async-start(), calls=%async_computation.24 | async-start | bytes 2359296 | tf_op jit(solution)/shard_map/reduce_scatter | solution.py:365
  578.7 254.9 %reduce-scatter.25.cloned.1.call-start = ((), (), s32[]{:S(2)}) async-start(), calls=%async_computation.25 | async-start | bytes 589824
  578.8 7.2 copy-start.17
  578.8 7.2 copy-start.19
  578.8 7.2 copy-start.24
  578.8 7.2 copy-start.26
  585.7 316.0 %reduce-scatter.21.cloned.1.call-start = ((), (), s32[]{:S(2)}) async-start(), calls=%async_computation.23 | async-start | bytes 1769472 | tf_op jit(solution)/shard_map/reduce_scatter | solution.py:377
  594.4 1.2 copy-start.4
  595.6 15.6 %copy-start.21 = (f32[256]{0:T(256)S(1)}, f32[256]{0:T(256)}, u32[]{:S(2)}) copy-start(f32[256]{0:T(256)} %param.20) | copy-start | bytes 3076
  601.1 1.0 copy-start.1
  602.1 50.6 %all-to-all-start.1 = ((bf16[8,256,256]{2,1,0:T(8,128)(2,1)}), bf16[8,256,256]{2,1,0:T(8,128)(2,1)S(1)}, u32[]{:S(2)}, u32[]{:S(2)}) async-start(bf16[8,256,256]{2,1,0:T(8,128)(2,1)} %bitcast.81), calls=%async_computation.3 | async-start | bytes 2097152 | tf_op jit(solution)/shard_map/all_to_all | solution.py:273
  633.7 1.0 copy-start
  652.7 290.5 %all-to-all-start.3 = ((bf16[8,256,256]{2,1,0:T(8,128)(2,1)}), bf16[8,256,256]{2,1,0:T(8,128)(2,1)}, u32[]{:S(2)}, u32[]{:S(2)}) async-start(bf16[8,256,256]{2,1,0:T(8,128)(2,1)} %bitcast.80), calls=%async_computation.7 | async-start | bytes 2097152 | tf_op jit(solution)/shard_map/all_to_all | solution.py:273
Sparse Core Ops, SparseCore 0:
  11.0 6.1 sort.28.cloned.1.call-done
  63.7 33.9 all-gather.7
  100.3 44.4 all-gather.9
  173.2 45.5 reduce-scatter.12
  221.4 61.2 all-gather.13
  284.7 32.6 all-gather.11
  320.0 50.3 all-gather.15
  371.9 33.1 all-gather.17
  427.2 44.5 reduce-scatter.16
  478.2 34.4 all-gather.19
  515.3 44.3 reduce-scatter.14
  562.1 44.3 reduce-scatter.18
  610.1 87.7 reduce-scatter.26
  701.3 67.3 reduce-scatter.22
  771.8 61.7 reduce-scatter.24
  836.9 64.7 reduce-scatter.20
  (1 shorter events, 0.0 us)

commit v2 on v1

--- a/solution.py
+++ b/solution.py
@@ -1,3 +1,5 @@
+import functools
+
 import jax
 import jax.numpy as jnp
 from jax import lax
@@ -213,6 +215,244 @@
     return start, first
 
 
+MESH = pl.DeviceIdType.MESH
+
+
+def neighbours():
+    own = lax.axis_index("narrow")
+    beside = own + 1 - 2 * (own % 2)
+    across = (own + 2) % 4
+    return own, beside, across, (beside + 2) % 4
+
+
+def greet(*peers):
+    barrier = pltpu.get_barrier_semaphore()
+    for peer in peers:
+        pl.semaphore_signal(barrier, inc=1, device_id={"narrow": peer}, device_id_type=MESH)
+    pl.semaphore_wait(barrier, len(peers))
+
+
+def push(src, dst, send_sem, recv_sem, peer):
+    return pltpu.make_async_remote_copy(
+        src_ref=src, dst_ref=dst, send_sem=send_sem, recv_sem=recv_sem, device_id={"narrow": peer}, device_id_type=MESH
+    )
+
+
+def chunk(base, k, rows):
+    return pl.ds(pl.multiple_of(base + k * rows, rows), rows)
+
+
+def rows_norm(x):
+    mean = jnp.mean(x, axis=1, keepdims=True)
+    scale = lax.rsqrt(jnp.mean(x * x, axis=1, keepdims=True) - mean * mean + NORM_EPS)
+    return (x - mean) * scale, scale
+
+
+def project_kernel(rows, mixed_ref, weight_ref, routed_ref, vec_ref, act_ref, middle_ref,
+                   a_out, a_in, x_out, x_in, b_out, b_in, sends, recvs):
+    own, beside, across, corner = neighbours()
+    share = middle_ref.shape[0]
+    count = share // rows
+    greet(beside, across)
+
+    def partial(quarter, k):
+        at = chunk(quarter * share, k, rows)
+        return jnp.dot(mixed_ref[at, :], weight_ref[...], preferred_element_type=jnp.float32)
+
+    def copies(kind, k, src, dst, peer):
+        at = chunk(0, k, rows)
+        return push(src.at[at, :], dst.at[at, :], sends.at[kind, k], recvs.at[kind, k], peer)
+
+    def spread(kind, quarter, k, peer):
+        at = chunk(quarter * share, k, rows)
+        return push(act_ref.at[at, :], act_ref.at[at, :], sends.at[kind, k], recvs.at[kind, k], peer)
+
+    def first(k, carry):
+        a_out[chunk(0, k, rows), :] = partial(corner, k).astype(jnp.bfloat16)
+        copies(0, k, a_out, a_in, beside).start()
+        return carry
+
+    def second(k, carry):
+        part = partial(across, k)
+        copies(0, k, a_out, a_in, beside).wait_recv()
+        at = chunk(0, k, rows)
+        x_out[at, :] = (part + a_in[at, :].astype(jnp.float32)).astype(jnp.bfloat16)
+        copies(1, k, x_out, x_in, across).start()
+        return carry
+
+    def third(k, carry):
+        b_out[chunk(0, k, rows), :] = partial(beside, k).astype(jnp.bfloat16)
+        copies(2, k, b_out, b_in, beside).start()
+        return carry
+
+    def fourth(k, carry):
+        part = partial(own, k)
+        at = chunk(0, k, rows)
+        copies(2, k, b_out, b_in, beside).wait_recv()
+        part += b_in[at, :].astype(jnp.float32)
+        copies(1, k, x_out, x_in, across).wait_recv()
+        part += x_in[at, :].astype(jnp.float32)
+        middle = part + routed_ref[at, :].astype(jnp.float32) + vec_ref[0:1, :]
+        middle_ref[at, :] = middle
+        normed, _ = rows_norm(middle)
+        act_ref[chunk(own * share, k, rows), :] = (normed * vec_ref[1:2, :] + vec_ref[2:3, :]).astype(jnp.bfloat16)
+        spread(3, own, k, across).start()
+        spread(4, own, k, beside).start()
+        return carry
+
+    def fifth(k, carry):
+        spread(3, across, k, across).wait_recv()
+        spread(5, across, k, beside).start()
+        return carry
+
+    def last(k, carry):
+        copies(0, k, a_out, a_in, beside).wait_send()
+        copies(1, k, x_out, x_in, across).wait_send()
+        copies(2, k, b_out, b_in, beside).wait_send()
+        spread(3, own, k, across).wait_send()
+        spread(4, own, k, beside).wait_send()
+        spread(5, across, k, beside).wait_send()
+        spread(4, beside, k, beside).wait_recv()
+        spread(5, corner, k, beside).wait_recv()
+        return carry
+
+    for stage in (first, second, third, fourth, fifth, last):
+        lax.fori_loop(0, count, stage, 0)
+
+
+def project_and_norm(mixed, out_full, routed_mine, vectors, rows=128):
+    total, width = mixed.shape[0], out_full.shape[1]
+    share = routed_mine.shape[0]
+    count = share // rows
+    buffer = pltpu.VMEM((share, width), jnp.bfloat16)
+    vmem = pl.BlockSpec(memory_space=pltpu.VMEM)
+    return pl.pallas_call(
+        functools.partial(project_kernel, rows),
+        out_shape=(
+            jax.ShapeDtypeStruct((total, width), jnp.bfloat16),
+            jax.ShapeDtypeStruct((share, width), jnp.float32),
+        ),
+        in_specs=[vmem] * 4,
+        out_specs=(vmem, vmem),
+        scratch_shapes=[buffer] * 6 + [pltpu.SemaphoreType.DMA((6, count)), pltpu.SemaphoreType.DMA((6, count))],
+        compiler_params=pltpu.CompilerParams(collective_id=1, has_side_effects=True, vmem_limit_bytes=40 << 20),
+        cost_estimate=pl.CostEstimate(flops=30_000_000_000, bytes_accessed=16 << 20, transcendentals=0),
+        name="project_and_norm",
+    )(mixed, out_full, routed_mine, vectors)
+
+
+GELU_A = (2.0 / 3.141592653589793) ** 0.5
+GELU_B = 0.044715
+
+
+def mlp_kernel(rows, act_ref, grad_ref, up_ref, down_ref, bias_ref, middle_ref, vec_ref,
+               hidden_ref, gpre_ref, branch_ref, norm_ref,
+               a_out, a_in, x_out, x_in, b_out, b_in, sends, recvs):
+    own, beside, across, corner = neighbours()
+    share = middle_ref.shape[0]
+    count = share // rows
+    greet(beside, across)
+    norm_ref[...] = jnp.zeros_like(norm_ref)
+
+    def partial(quarter, k):
+        at = chunk(quarter * share, k, rows)
+        u = jnp.dot(act_ref[at, :], up_ref[...], preferred_element_type=jnp.float32) + bias_ref[0:1, :]
+        square = u * u
+        t = jnp.tanh(GELU_A * (u + GELU_B * square * u))
+        half = 0.5 * (1.0 + t)
+        hidden_ref[at, :] = (u * half).astype(jnp.bfloat16)
+        slope = half + 0.5 * u * (1.0 - t * t) * (GELU_A * (1.0 + (3.0 * GELU_B) * square))
+        back = lax.dot_general(grad_ref[at, :], down_ref[...], NT, preferred_element_type=jnp.float32)
+        gpre = (back * slope).astype(jnp.bfloat16)
+        gpre_ref[at, :] = gpre
+        return lax.dot_general(gpre, up_ref[...], NT, preferred_element_type=jnp.float32)
+
+    def copies(kind, k, src, dst, peer):
+        at = chunk(0, k, rows)
+        return push(src.at[at, :], dst.at[at, :], sends.at[kind, k], recvs.at[kind, k], peer)
+
+    def spread(kind, quarter, k, peer):
+        at = chunk(quarter * share, k, rows)
+        return push(branch_ref.at[at, :], branch_ref.at[at, :], sends.at[kind, k], recvs.at[kind, k], peer)
+
+    def outward(k, carry):
+        at = chunk(0, k, rows)
+        a_out[at, :] = partial(corner, k).astype(jnp.bfloat16)
+        copies(0, k, a_out, a_in, beside).start()
+        part = partial(across, k)
+        copies(0, k, a_out, a_in, beside).wait_recv()
+        x_out[at, :] = (part + a_in[at, :].astype(jnp.float32)).astype(jnp.bfloat16)
+        copies(1, k, x_out, x_in, across).start()
+        return carry
+
+    def inward(k, carry):
+        at = chunk(0, k, rows)
+        b_out[at, :] = partial(beside, k).astype(jnp.bfloat16)
+        copies(2, k, b_out, b_in, beside).start()
+        part = partial(own, k)
+        copies(2, k, b_out, b_in, beside).wait_recv()
+        part += b_in[at, :].astype(jnp.float32)
+        copies(1, k, x_out, x_in, across).wait_recv()
+        part += x_in[at, :].astype(jnp.float32)
+        normed, scale = rows_norm(middle_ref[at, :])
+        norm_ref[0:1, :] += jnp.sum(part * normed, axis=0, keepdims=True)
+        norm_ref[1:2, :] += jnp.sum(part, axis=0, keepdims=True)
+        scaled = part * vec_ref[1:2, :]
+        back = scale * (
+            scaled
+            - jnp.mean(scaled, axis=1, keepdims=True)
+            - normed * jnp.mean(scaled * normed, axis=1, keepdims=True)
+        )
+        rows_own = chunk(own * share, k, rows)
+        branch_ref[rows_own, :] = (grad_ref[rows_own, :].astype(jnp.float32) + back).astype(jnp.bfloat16)
+        spread(3, own, k, across).start()
+        spread(4, own, k, beside).start()
+        return carry
+
+    def forward(k, carry):
+        spread(3, across, k, across).wait_recv()
+        spread(5, across, k, beside).start()
+        return carry
+
+    def last(k, carry):
+        copies(0, k, a_out, a_in, beside).wait_send()
+        copies(1, k, x_out, x_in, across).wait_send()
+        copies(2, k, b_out, b_in, beside).wait_send()
+        spread(3, own, k, across).wait_send()
+        spread(4, own, k, beside).wait_send()
+        spread(5, across, k, beside).wait_send()
+        spread(4, beside, k, beside).wait_recv()
+        spread(5, corner, k, beside).wait_recv()
+        return carry
+
+    for stage in (outward, inward, forward, last):
+        lax.fori_loop(0, count, stage, 0)
+
+
+def mlp_both_ways(act_two, grad_full, up_full, down_full, up_bias, middle, vectors, rows=256):
+    total, width = act_two.shape
+    hidden = up_full.shape[1]
+    share = middle.shape[0]
+    count = share // rows
+    buffer = pltpu.VMEM((share, width), jnp.bfloat16)
+    vmem = pl.BlockSpec(memory_space=pltpu.VMEM)
+    return pl.pallas_call(
+        functools.partial(mlp_kernel, rows),
+        out_shape=(
+            jax.ShapeDtypeStruct((total, hidden), jnp.bfloat16),
+            jax.ShapeDtypeStruct((total, hidden), jnp.bfloat16),
+            jax.ShapeDtypeStruct((total, width), jnp.bfloat16),
+            jax.ShapeDtypeStruct((8, width), jnp.float32),
+        ),
+        in_specs=[vmem] * 7,
+        out_specs=(vmem,) * 4,
+        scratch_shapes=[buffer] * 6 + [pltpu.SemaphoreType.DMA((6, count)), pltpu.SemaphoreType.DMA((6, count))],
+        compiler_params=pltpu.CompilerParams(collective_id=2, has_side_effects=True, vmem_limit_bytes=60 << 20),
+        cost_estimate=pl.CostEstimate(flops=40_000_000_000, bytes_accessed=32 << 20, transcendentals=0),
+        name="mlp_both_ways",
+    )(act_two, grad_full, up_full, down_full, up_bias, middle, vectors)
+
+
 def pick_kernel(index_ref, *refs):
     count = len(refs) // 2
     rows = refs[0].shape[0]
@@ -323,37 +563,20 @@
     up_full = lax.all_gather(up_weight.astype(low), "wide", axis=0, tiled=True)
     down_full = lax.all_gather(down_weight.astype(low), "wide", axis=1, tiled=True)
 
-    routed_full = lax.all_gather(routed, "narrow", axis=1, tiled=True).astype(wide_type)
+    routed_low = lax.all_gather(routed, "narrow", axis=1, tiled=True)
+    routed_full = routed_low.astype(wide_type)
     mean_one, scale_one = row_stats(routed_full)
     act_one = ((routed_full - mean_one) * scale_one * vectors[0] + vectors[1]).astype(low)
     shift = jnp.concatenate([qv_bias[0], jnp.zeros((quarter,), wide_type), qv_bias[1]])
     proj = (jnp.dot(act_one, qkv_full, preferred_element_type=wide_type) + shift).astype(low)
     mixed, log_sums = attention_forward(proj, first, jnp.broadcast_to(start[:, None], (row_count, 128)))
-    branch = jnp.dot(mixed, out_full, preferred_element_type=wide_type).astype(low)
-    branch = lax.psum_scatter(branch, "narrow", scatter_dimension=0, tiled=True).astype(wide_type)
-    middle = mine(routed_full) + branch + vectors[4]
-    mean_two, scale_two = row_stats(middle)
-    normed_two = (middle - mean_two) * scale_two
-    act_two = lax.all_gather((normed_two * vectors[2] + vectors[3]).astype(low), "narrow", axis=0, tiled=True)
+    norm_rows = jnp.concatenate([vectors[4:5], vectors[2:4], jnp.zeros((5, D), wide_type)])
+    act_two, middle = project_and_norm(mixed, out_full, mine(routed_low), norm_rows)
 
     grad_full = lax.all_gather(routed_grad, "narrow", axis=1, tiled=True)
-    preact = jnp.dot(act_two, up_full, preferred_element_type=wide_type) + up_bias
-    gelu, gelu_back = jax.vjp(lambda u: jax.nn.gelu(u, approximate=True), preact)
-    hidden = gelu.astype(low)
-    grad_hidden = jnp.einsum("td,fd->tf", grad_full, down_full, preferred_element_type=wide_type)
-    grad_pre = gelu_back(grad_hidden)[0].astype(low)
-    grad_act_two = jnp.einsum("tf,df->td", grad_pre, up_full, preferred_element_type=wide_type).astype(low)
-    grad_act_two = lax.psum_scatter(grad_act_two, "narrow", scatter_dimension=0, tiled=True).astype(wide_type)
-    scaled = grad_act_two * vectors[2]
-    back_two = scale_two * (
-        scaled
-        - jnp.mean(scaled, axis=1, keepdims=True)
-        - normed_two * jnp.mean(scaled * normed_two, axis=1, keepdims=True)
+    hidden, grad_pre, branch_full, norm_sums = mlp_both_ways(
+        act_two, grad_full, up_full, down_full, jnp.broadcast_to(up_bias[None], (8, up_bias.shape[0])), middle, norm_rows
     )
-    grad_branch = (mine(grad_full).astype(wide_type) + back_two).astype(low)
-    branch_full = lax.all_gather(grad_branch, "narrow", axis=0, tiled=True)
-    gain_two_grad = jnp.sum(grad_act_two * normed_two, axis=0)
-    bias_two_grad = jnp.sum(grad_act_two, axis=0)
 
     held = jnp.arange(parts, dtype=jnp.int32)[:, None, None] == part
     kept = jnp.where(held, (middle + vectors[5])[None], 0.0).reshape(row_count, D)
@@ -387,7 +610,7 @@
     (input_sent,) = pick(arrive_rows, grad_input)
     (input_grad,) = place(send_rows, exchanged(input_sent))
 
-    norm_two = lax.psum(jnp.stack([gain_two_grad, bias_two_grad]), ("wide", "narrow"))
+    norm_two = lax.psum(norm_sums[:2], ("wide", "narrow"))
     norm_two = lax.dynamic_slice_in_dim(norm_two, part * quarter, quarter, 1)
     middle_sums = lax.psum(
         (

time: 966 us -> 801 us (0.83)
  waiting for transfers between devices: 492 us -> 283 us
  Pallas kernels: 89.6 us -> 214 us
  matrix products: 95.6 us -> 57.8 us
  blocking collectives: 167 us -> 138 us
  other arithmetic: 42 us -> 27.5 us
    pallas_call x0 -> x2, Pallas kernels: none -> 115 us  [the longest x1 63.9 us: mlp_both_ways(): pl.pallas_call(functools.partial(mlp_kernel, rows), out_shape=(jax.ShapeD...]
    reduce_scatter x2 -> x0, waiting for transfers between devices: 80.5 us -> none  [the longest x1 44.5 us: local(): lax.psum_scatter(grad_act_two, 'narrow', scatter_dimension=0, tiled=True)]
    all_gather x3 -> x1, waiting for transfers between devices: 56.9 us -> 0.02 us  [local(): routed_low = lax.all_gather(routed, 'narrow', axis=1, tiled=True)]
    all_to_all x1 -> x0, blocking collectives: 48.8 us -> none  [exchanged(): lax.all_to_all(rows_out, 'wide', split_axis=0, concat_axis=0, tiled=True)]
    dot_general x4 -> x0, matrix products: 33.8 us -> none  [the longest x1 13.7 us: local(): jnp.einsum('td,fd->tf', grad_full, down_full, preferred_element_type=wide...]
    all_gather x1, waiting for transfers between devices: 43.2 us -> 11.3 us  [local(): lax.all_gather(qkv_weight.astype(low).reshape(qkv_weight.shape[0], 3 * qu...]
    all_gather x1, waiting for transfers between devices: 42.4 us -> 18 us  [local(): lax.all_gather(down_weight.astype(low), 'wide', axis=1, tiled=True)]
    all_gather x1, blocking collectives: 27.7 us -> 43.9 us  [local(): lax.all_gather(out_weight.astype(low), 'wide', axis=1, tiled=True)]
  transfers between devices with their start and end apart: 18 -> 15, of which waited for: 13 -> 8; matrix products, arithmetic and copies ran while one was open for 12% -> 11% of each run, Pallas kernels for 6% -> 17%
where the time goes in v2:
time: 801 us; the launch traced here: 793 us
  waiting for transfers between devices  283 us (35%)
  Pallas kernels  214 us (27%)
  blocking collectives  138 us (17%)
  matrix products  57.8 us (7%)
  local copies, waits for them, and re-layouts  34.7 us (4%)
  other arithmetic  27.5 us (3%)
  starting transfers between devices  22.5 us (3%)
  between operations  15.5 us (2%)
    unnamed x13, waiting for transfers between devices  69 us
    reduce_scatter x1, waiting for transfers between devices, local(): lax.psum_scatter(up_grad, 'wide', scatter_dimension=0, tiled=True)  68.9 us
    pallas_call x1, Pallas kernels, mlp_both_ways(): pl.pallas_call(functools.partial(mlp_kernel, rows), out_shape=(jax.ShapeD...  63.9 us
    reduce_scatter x1, waiting for transfers between devices, local(): lax.psum_scatter(qkv_grad, 'wide', scatter_dimension=0, tiled=True)  53.8 us
    pallas_call x1, Pallas kernels, project_and_norm(): pl.pallas_call(functools.partial(project_kernel, rows), out_shape=(jax.Sh...  51.4 us
    pallas_call x8, Pallas kernels, permuted(): pl.pallas_call(kernel, out_shape=[jax.ShapeDtypeStruct(a.shape, a.dtype)...  43.9 us
    all_gather x1, blocking collectives, local(): lax.all_gather(out_weight.astype(low), 'wide', axis=1, tiled=True)  43.9 us
    psum x1, blocking collectives, local(): norm_two = lax.psum(norm_sums[:2], ('wide', 'narrow'))  43.1 us
  transfers between devices with their start and end apart: 15, of which 8 were waited for; matrix products, arithmetic and copies ran while one was open for 11% of the time, Pallas kernels for 17%

profile of v2, /device:TPU:0, one launch (start us, length us, event | category | flops | bytes accessed | tf_op | source)
XLA Modules:
  0.0 793.2 jit_solution(1692518740062268703)
XLA Ops:
  7.2 0.9 reshape.99
  8.8 8.5 %sort.26.cloned.1.call-done = s32[8,2048]{1,0:T(8,128)} async-done(((s32[8,2048]{1,0:T(8,128)}), s32[8,2048]{1,0:T(8,128)}) %sort.26.cloned.1.call-update) | async-done | bytes 65552 | tf_op jit(solution)/shard_map/jit(sort)/sort | solution.py:506
  18.1 1.2 copy-done.10
  19.3 6.2 pick_rows.4
  25.5 7.3 all-to-all-start
  32.9 5.0 sort.24
  37.9 20.6 %all-to-all-done = bf16[8,256,256]{2,1,0:T(8,128)(2,1)S(1)} async-done(((bf16[8,256,256]{2,1,0:T(8,128)(2,1)}), bf16[8,256,256]{2,1,0:T(8,128)(2,1)S(1)}, u32[]{:S(2)}, u32[]{:S(2)}) %all-to-all-start) | async-done | bytes 1048608 | tf_op jit(solution)/shard_map/all_to_all | solution.py:513
  58.6 4.9 place_rows.4
  63.5 1.8 copy.37
  67.1 6.2 pick_rows.5
  73.3 3.6 all-to-all-start.1
  77.5 5.5 all_gather.22
  83.3 43.9 %all_gather.24.weight_ref = bf16[256,1024]{1,0:T(8,128)(2,1)} all-gather(bf16[256,128]{1,0:T(8,128)(2,1)S(1)} %convert_element_type.81), channel_id=1, replica_groups=mesh['wide'=8,'narrow'=4] {'wide'}, dimensions={1}, use_global_device_ids=true | all-gather | bytes 589824 | tf_op jit(solution)/shard_map/all_gather | solution.py:562
  127.2 4.8 place_rows.5
  132.1 1.3 constant_dynamic-slice_fusion.1.routed_ref
  133.4 3.4 convert_reduce_fusion
  136.9 11.3 %all-gather.8.cloned.1.call-done = bf16[1024,768]{0,1:T(8,128)(2,1)} async-done(((bf16[128,768]{0,1:T(8,128)(2,1)}), bf16[1024,768]{0,1:T(8,128)(2,1)}) %all-gather.8.cloned.1.call-update) | async-done | bytes 1572880 | tf_op jit(solution)/shard_map/all_gather | solution.py:561
  148.2 6.9 add_convert_fusion.q_ref.k_ref.v_ref
  155.5 20.9 %attn_fwd.1 = (bf16[2048,256]{1,0:T(8,128)(2,1)S(1)}, f32[8,2048]{1,0:T(8,128)S(1)}) custom-call(s32[8]{0:T(128)S(1)} %and_select_fusion.first_ref, bf16[2048,768]{1,0:T(8,128)(2,1)S(1)} %add_convert_fusion.q_ref.k_ref.v_ref, bf16[2048,768]{1,0:T(8,128)(2,1)S(1)} %add_convert_fusion.q_ref.k_ref.v_ref, ...), custom_call_target="tpu_custom_call" | custom-call | flops 16000000000 | bytes 8388608 | tf_op jit(solution)/shard_map/attn_fwd/pallas_call | solution.py:85
  176.5 51.4 %project_and_norm.1 = (bf16[2048,1024]{1,0:T(8,128)(2,1)S(1)}, f32[512,1024]{1,0:T(8,128)S(1)}) custom-call(bf16[2048,256]{1,0:T(8,128)(2,1)S(1)} %get-tuple-element.28.mixed_ref.o_ref, bf16[256,1024]{1,0:T(8,128)(2,1)S(1)} %copy-done.3, bf16[512,1024]{1,0:T(8,128)(2,1)S(1)} %constant_dynamic-slice_fusion.1.routed_ref, f32[8,1024]{1,0:T(8,128)S(1)} %maximum_maximum_fusion.vec_ref), custom_call_target="tpu_custom_call" | custom-call | flops 30000001024 | bytes 16777216 | tf_op jit(solution)/shard_map/project_and_norm/pallas_call | solution.py:329
  227.9 1.9 copy-done.15
  229.8 1.5 broadcast_add_fusion
  231.4 18.0 %all-gather.14.cloned.1.call-done.down_ref = bf16[1024,1024]{1,0:T(8,128)(2,1)} async-done(((bf16[1024,128]{1,0:T(8,128)(2,1)}), bf16[1024,1024]{1,0:T(8,128)(2,1)}) %all-gather.14.cloned.1.call-update) | async-done | bytes 2097168 | tf_op jit(solution)/shard_map/all_gather | solution.py:564
  249.4 35.2 %all-gather.10.cloned.1.call-done.grad_ref = bf16[2048,1024]{1,0:T(8,128)(2,1)} async-done(((bf16[2048,256]{1,0:T(8,128)(2,1)}), bf16[2048,1024]{1,0:T(8,128)(2,1)}) %all-gather.10.cloned.1.call-update) | async-done | bytes 4194320 | tf_op jit(solution)/shard_map/all_gather | solution.py:576
  285.2 63.9 %mlp_both_ways.1 = (bf16[2048,1024]{1,0:T(8,128)(2,1)}, bf16[2048,1024]{1,0:T(8,128)(2,1)}, bf16[2048,1024]{1,0:T(8,128)(2,1)}, f32[8,1024]{1,0:T(8,128)}) custom-call(bf16[2048,1024]{1,0:T(8,128)(2,1)} %copy-done.15, bf16[2048,1024]{1,0:T(8,128)(2,1)} %all-gather.10.cloned.1.call-done.grad_ref, bf16[1024,1024]{1,0:T(8,128)(2,1)} %all-gather.12.cloned.1.call-done.up_ref, ...), custom_call_target="tpu_custom_call" | custom-call | flops 40000000000 | bytes 33554432 | tf_op jit(solution)/shard_map/mlp_both_ways/pallas_call | solution.py:439
  349.1 10.1 %fusion.6 = bf16[2048,1024]{1,0:T(8,128)(2,1)} fusion(f32[512,1024]{1,0:T(8,128)} %broadcast_add_fusion, pred[2048]{0:T(1024)(128)(4,1)S(1)} %bitcast.95, bf16[2048,1024]{1,0:T(8,128)(2,1)} %get-tuple-element.31, bf16[1024,1024]{1,0:T(8,128)(2,1)} %all-gather.14.cloned.1.call-done.down_ref), kind=kOutput, calls=%fused_computation.10 | convolution fusion | flops 4301258752 | bytes 12584960 | tf_op jit(solution)/shard_map/dot_general | solution.py:583
  359.2 1.0 copy-done.4
  360.2 3.6 convolution_convert_fusion.1.do_ref
  363.9 33.6 %attn_bwd.1 = (bf16[2048,256]{1,0:T(8,128)(2,1)S(1)}, bf16[2048,256]{1,0:T(8,128)(2,1)S(1)}, bf16[2048,256]{1,0:T(8,128)(2,1)S(1)}) custom-call(s32[8]{0:T(128)S(1)} %and_select_fusion.first_ref, bf16[2048,768]{1,0:T(8,128)(2,1)S(1)} %copy-done.17, bf16[2048,768]{1,0:T(8,128)(2,1)S(1)} %copy-done.17, bf16[2048,768]{1,0:T(8,128)(2,1)S(1)} %copy-done.17, ...), custom_call_target="tpu_custom_call" | custom-call | flops 40000000000 | bytes 8388608 | tf_op jit(solution)/shard_map/attn_bwd/pallas_call | solution.py:179
  397.7 1.6 copy-done.20
  399.5 4.9 convolution_convert_fusion
  404.5 4.3 convolution_convert_fusion.5
  408.8 2.0 copy.40
  411.1 9.2 %convolution_convert_fusion.4 = bf16[1024,768]{1,0:T(8,128)(2,1)} fusion(bf16[2048,768]{1,0:T(8,128)(2,1)} %copy-done.20, bf16[2048,1024]{1,0:T(8,128)(2,1)} %all-gather.6.cloned.1.call-done, f32[1024]{0:T(1024)S(1)} %bitcast.92, f32[1024]{0:T(1024)S(1)} %bitcast.94, f32[2048]{0:T(1024)S(1)} %copy-done.25, f32[2048]{0:T(1024)S(1)} %copy-done.23), kind=kOutput, calls=%fused_computation.34 | convolution fusion | flops 3234594816 | bytes 8937472 | tf_op jit(solution)/shard_map/td,tc->dc/dot_general | solution.py:599
  420.4 9.4 %convolution_convert_fusion.2 = bf16[1024,1024]{1,0:T(8,128)(2,1)} fusion(bf16[2048,1024]{1,0:T(8,128)(2,1)} %get-tuple-element.31, bf16[2048,1024]{1,0:T(8,128)(2,1)} %all-gather.10.cloned.1.call-done.grad_ref), kind=kOutput, calls=%fused_computation.32 | convolution fusion | flops 4296015872 | bytes 10485760 | tf_op jit(solution)/shard_map/tf,td->fd/dot_general | solution.py:585
  429.8 3.9 copy.42
  434.1 9.4 %convolution_convert_fusion.3 = bf16[1024,1024]{1,0:T(8,128)(2,1)} fusion(bf16[2048,1024]{1,0:T(8,128)(2,1)} %copy-done.15, bf16[2048,1024]{1,0:T(8,128)(2,1)} %get-tuple-element.38), kind=kOutput, calls=%fused_computation.33 | convolution fusion | flops 4296015872 | bytes 10485760 | tf_op jit(solution)/shard_map/td,tf->df/dot_general | solution.py:586
  443.6 1.2 copy-done.12
  444.8 5.5 pick_rows.6
  450.3 1.0 copy-done.2
  451.3 6.4 all-to-all-start.2
  457.7 2.6 fusion.14
  460.4 10.8 %psum.56 = f32[2,2048]{1,0:T(2,128)S(1)} all-reduce(f32[2,2048]{1,0:T(2,128)S(1)} %pad_maximum_fusion), channel_id=1, replica_groups=mesh['wide'=8,'narrow'=4] {'narrow'}, use_global_device_ids=true, to_apply=%region_10.11 | all-reduce | flops 4096 | bytes 32768 | tf_op jit(solution)/shard_map/psum | solution.py:604
  471.2 3.5 convert_reduce_fusion.3
  474.7 5.5 pick_rows.7
  480.2 1.0 copy-done.1
  481.2 6.6 all-to-all-done.2
  487.7 4.2 all-to-all-start.3
  492.0 1.5 convert_reduce_fusion.4
  493.5 0.8 slice.53
  494.3 43.1 %psum.61 = f32[2,1024]{1,0:T(2,128)S(1)} all-reduce(f32[2,1024]{1,0:T(2,128)S(1)} %slice.53), channel_id=1, replica_groups=mesh['wide'=8,'narrow'=4] {'wide','narrow'}, use_global_device_ids=true, to_apply=%region_22.23 | all-reduce | flops 2048 | bytes 16384 | tf_op jit(solution)/shard_map/psum | solution.py:613
  538.4 2.9 convert_reduce_fusion.1
  541.3 0.9 copy.41
  542.9 53.8 %reduce-scatter.15.cloned.1.call-done = bf16[128,768]{1,0:T(8,128)(2,1)} async-done(((bf16[1024,768]{1,0:T(8,128)(2,1)}), bf16[128,768]{1,0:T(8,128)(2,1)}) %reduce-scatter.15.cloned.1.call-update) | async-done | bytes 196624 | tf_op jit(solution)/shard_map/reduce_scatter | solution.py:600
  596.7 1.1 copy.38
  597.8 0.9 copy.39
  598.7 68.8 %reduce-scatter.21.cloned.1.call-done = bf16[128,1024]{1,0:T(8,128)(2,1)} async-done(((bf16[1024,1024]{1,0:T(8,128)(2,1)}), bf16[128,1024]{1,0:T(8,128)(2,1)}) %reduce-scatter.21.cloned.1.call-update) | async-done | bytes 262160
  667.4 1.1 copy.43
  668.6 0.8 convert_element_type.100
  669.4 68.9 %reduce-scatter.17.cloned.1.call-done = bf16[128,1024]{1,0:T(8,128)(2,1)} async-done(((bf16[1024,1024]{1,0:T(8,128)(2,1)}), bf16[128,1024]{1,0:T(8,128)(2,1)}) %reduce-scatter.17.cloned.1.call-update) | async-done | bytes 262160 | tf_op jit(solution)/shard_map/reduce_scatter | solution.py:588
  738.3 1.8 convert_element_type.97
  740.1 34.9 %all-reduce = (f32[256]{0:T(256)}, f32[256]{0:T(256)}, f32[2,256]{1,0:T(2,128)}, f32[256]{0:T(256)}, f32[1024]{0:T(1024)}, /*index=5*/f32[256]{0:T(256)}) all-reduce(f32[256]{0:T(256)S(1)} %get-tuple-element.97, f32[256]{0:T(256)S(1)} %get-tuple-element.100, ...), channel_id=1, replica_groups=mesh['wide'=8,'narrow'=4] {'wide'}, use_global_device_ids=true, to_apply=%region_12.13 | all-reduce | flops 2560 | bytes 20480 | tf_op jit(solution)/shard_map/psum | solution.py:623
  775.0 4.8 place_rows.6
  779.8 6.1 place_rows.7
  (150 shorter events, 8.1 us)
Async XLA Ops:
  7.2 10.2 %sort.26.cloned.1.call-start = ((), (), s32[]{:S(2)}) async-start(), calls=%async_computation.21 | async-start | bytes 196640 | tf_op jit(solution)/shard_map/jit(sort)/sort | solution.py:506
  18.1 1.2 copy-start.10
  19.3 47.7 %copy-start.5 = (s32[8,2048]{1,0:T(8,128)}, s32[8,2048]{1,0:T(8,128)S(1)}, u32[]{:S(2)}) copy-start(s32[8,2048]{1,0:T(8,128)S(1)} %broadcast_in_dim.91.index_ref) | copy-start | bytes 196612
  25.5 33.1 %all-to-all-start = ((bf16[8,256,256]{2,1,0:T(8,128)(2,1)}), bf16[8,256,256]{2,1,0:T(8,128)(2,1)S(1)}, u32[]{:S(2)}, u32[]{:S(2)}) async-start(bf16[8,256,256]{2,1,0:T(8,128)(2,1)} %bitcast.5), calls=%async_computation | async-start | bytes 2097152 | tf_op jit(solution)/shard_map/all_to_all | solution.py:513
  32.8 99.3 %all-gather.6.cloned.1.call-start = ((), (), s32[]{:S(2)}) async-start(), calls=%async_computation.10 | async-start | bytes 5242880 | tf_op jit(solution)/shard_map/all_gather | solution.py:566
  58.6 68.6 %copy-start.7 = (s32[8,2048]{1,0:T(8,128)}, s32[8,2048]{1,0:T(8,128)S(1)}, u32[]{:S(2)}) copy-start(s32[8,2048]{1,0:T(8,128)S(1)} %broadcast_in_dim.92.index_ref) | copy-start | bytes 196612
  58.6 6.9 copy-start.18
  58.6 7.7 copy-start.19
  58.6 8.4 %copy-start.11 = (bf16[2048,256]{1,0:T(8,128)(2,1)S(1)}, bf16[2048,256]{1,0:T(8,128)(2,1)}, u32[]{:S(2)}) copy-start(bf16[2048,256]{1,0:T(8,128)(2,1)} %refs_0_.3) | copy-start | bytes 3145732
  63.5 84.7 %all-gather.8.cloned.1.call-start = ((), (), s32[]{:S(2)}) async-start(), calls=%async_computation.11 | async-start | bytes 1769472 | tf_op jit(solution)/shard_map/all_gather | solution.py:561
  65.4 166.0 %all-gather.12.cloned.1.call-start = ((), (), s32[]{:S(2)}) async-start(), calls=%async_computation.13 | async-start | bytes 2359296 | tf_op jit(solution)/shard_map/all_gather | solution.py:563
  66.2 183.2 %all-gather.14.cloned.1.call-start = ((), (), s32[]{:S(2)}) async-start(), calls=%async_computation.14 | async-start | bytes 2359296 | tf_op jit(solution)/shard_map/all_gather | solution.py:564
  67.0 10.0 %copy-start.40 = (s32[1,4]{1,0:T(1,128)S(1)}, s32[1,4]{1,0:T(1,128)}, u32[]{:S(2)}) copy-start(s32[1,4]{1,0:T(1,128)} %param.19) | copy-start | bytes 52
  67.0 10.4 %copy-start.26 = (f32[256]{0:T(256)S(1)}, f32[256]{0:T(256)}, u32[]{:S(2)}) copy-start(f32[256]{0:T(256)} %param.20) | copy-start | bytes 3076
  67.1 10.4 %copy-start.34 = (f32[256]{0:T(256)S(1)}, f32[256]{0:T(256)}, u32[]{:S(2)}) copy-start(f32[256]{0:T(256)} %param.21) | copy-start | bytes 3076
  67.1 10.4 %copy-start.35 = (f32[256]{0:T(256)S(1)}, f32[256]{0:T(256)}, u32[]{:S(2)}) copy-start(f32[256]{0:T(256)} %param.26) | copy-start | bytes 3076
  67.1 10.4 %copy-start.36 = (f32[256]{0:T(256)S(1)}, f32[256]{0:T(256)}, u32[]{:S(2)}) copy-start(f32[256]{0:T(256)} %param.27) | copy-start | bytes 3076
  67.1 10.4 %copy-start.37 = (f32[256]{0:T(256)S(1)}, f32[256]{0:T(256)}, u32[]{:S(2)}) copy-start(f32[256]{0:T(256)} %param.25) | copy-start | bytes 3076
  67.1 10.4 %copy-start.38 = (f32[256]{0:T(256)S(1)}, f32[256]{0:T(256)}, u32[]{:S(2)}) copy-start(f32[256]{0:T(256)} %param.31) | copy-start | bytes 3076
  67.1 15.9 %copy-start.21 = (f32[256,128]{1,0:T(8,128)S(1)}, f32[256,128]{1,0:T(8,128)}, u32[]{:S(2)}) copy-start(f32[256,128]{1,0:T(8,128)} %param.24) | copy-start | bytes 393220
  67.1 16.0 %copy-start.33 = (f32[2,256]{1,0:T(2,128)S(1)}, f32[2,256]{1,0:T(2,128)}, u32[]{:S(2)}) copy-start(f32[2,256]{1,0:T(2,128)} %param.23) | copy-start | bytes 6148
  73.3 53.8 %all-to-all-start.1 = ((bf16[8,256,256]{2,1,0:T(8,128)(2,1)}), bf16[8,256,256]{2,1,0:T(8,128)(2,1)S(1)}, u32[]{:S(2)}, u32[]{:S(2)}) async-start(bf16[8,256,256]{2,1,0:T(8,128)(2,1)} %bitcast.18), calls=%async_computation.1 | async-start | bytes 2097152 | tf_op jit(solution)/shard_map/all_to_all | solution.py:513
  76.9 207.6 %all-gather.10.cloned.1.call-start = ((), (), s32[]{:S(2)}) async-start(), calls=%async_computation.12 | async-start | bytes 5242880 | tf_op jit(solution)/shard_map/all_gather | solution.py:576
  83.2 65.0 %copy-start.29 = (f32[1,1024]{1,0:T(1,128)}, f32[1,1024]{1,0:T(1,128)S(1)}, u32[]{:S(2)}) copy-start(f32[1,1024]{1,0:T(1,128)S(1)} %get-tuple-element.111) | copy-start | bytes 12292
  83.2 65.0 %copy-start.31 = (f32[1,1024]{1,0:T(1,128)}, f32[1,1024]{1,0:T(1,128)S(1)}, u32[]{:S(2)}) copy-start(f32[1,1024]{1,0:T(1,128)S(1)} %get-tuple-element.112) | copy-start | bytes 12292
  83.3 93.2 %copy-start.9 = (f32[8,1024]{1,0:T(8,128)}, f32[8,1024]{1,0:T(8,128)S(1)}, u32[]{:S(2)}) copy-start(f32[8,1024]{1,0:T(8,128)S(1)} %maximum_maximum_fusion.vec_ref) | copy-start | bytes 98308
  132.0 311.5 %reduce-scatter.11.cloned.1.call-start = ((), (), s32[]{:S(2)}) async-start(), calls=%async_computation.15 | async-start | bytes 5242880 | tf_op jit(solution)/shard_map/reduce_scatter | solution.py:584
  136.9 18.3 %copy-start.22 = (f32[2048]{0:T(1024)}, f32[2048]{0:T(1024)S(1)}, u32[]{:S(2)}) copy-start(f32[2048]{0:T(1024)S(1)} %get-tuple-element.117) | copy-start | bytes 24580
  136.9 18.3 %copy-start.24 = (f32[2048]{0:T(1024)}, f32[2048]{0:T(1024)S(1)}, u32[]{:S(2)}) copy-start(f32[2048]{0:T(1024)S(1)} %get-tuple-element.118) | copy-start | bytes 24580
  155.2 21.3 %copy-start.16 = (bf16[2048,768]{1,0:T(8,128)(2,1)}, bf16[2048,768]{1,0:T(8,128)(2,1)S(1)}, u32[]{:S(2)}) copy-start(bf16[2048,768]{1,0:T(8,128)(2,1)S(1)} %add_convert_fusion.q_ref.k_ref.v_ref) | copy-start | bytes 9437188
  155.5 21.0 %copy-start.3 = (bf16[256,1024]{1,0:T(8,128)(2,1)S(1)}, bf16[256,1024]{1,0:T(8,128)(2,1)}, u32[]{:S(2)}) copy-start(bf16[256,1024]{1,0:T(8,128)(2,1)} %all_gather.24.weight_ref) | copy-start | bytes 1572868
  176.4 51.5 %copy-start.13 = (bf16[2048,256]{1,0:T(8,128)(2,1)}, bf16[2048,256]{1,0:T(8,128)(2,1)S(1)}, u32[]{:S(2)}) copy-start(bf16[2048,256]{1,0:T(8,128)(2,1)S(1)} %get-tuple-element.28.mixed_ref.o_ref) | copy-start | bytes 3145732
  227.9 1.9 copy-start.15
  227.9 57.3 %copy-start = (f32[512,1024]{1,0:T(8,128)}, f32[512,1024]{1,0:T(8,128)S(1)}, u32[]{:S(2)}) copy-start(f32[512,1024]{1,0:T(8,128)S(1)} %get-tuple-element.30.middle_ref) | copy-start | bytes 6291460
  227.9 56.7 %copy-start.28 = (f32[1024]{0:T(1024)S(1)}, f32[1024]{0:T(1024)}, u32[]{:S(2)}) copy-start(f32[1024]{0:T(1024)} %param.29) | copy-start | bytes 12292
  359.2 1.0 copy-start.4
  359.2 98.5 %reduce-scatter.13.cloned.1.call-start = ((), (), s32[]{:S(2)}) async-start(), calls=%async_computation.16 | async-start | bytes 5242880 | tf_op jit(solution)/shard_map/reduce_scatter | solution.py:598
  360.2 3.7 copy-start.14
  360.2 3.7 copy-start.17
  397.4 2.0 copy-start.39
  397.7 1.6 copy-start.20
  404.4 6.7 copy-start.23
  404.4 6.7 copy-start.25
  404.4 6.7 copy-start.30
  404.4 6.7 copy-start.32
  404.4 136.9 %reduce-scatter.19.cloned.1.call-start = ((), (), s32[]{:S(2)}) async-start(), calls=%async_computation.19 | async-start | bytes 589824
  410.8 185.9 %reduce-scatter.15.cloned.1.call-start = ((), (), s32[]{:S(2)}) async-start(), calls=%async_computation.17 | async-start | bytes 1769472 | tf_op jit(solution)/shard_map/reduce_scatter | solution.py:600
  420.4 247.1 %reduce-scatter.21.cloned.1.call-start = ((), (), s32[]{:S(2)}) async-start(), calls=%async_computation.20 | async-start | bytes 2359296
  433.8 304.5 %reduce-scatter.17.cloned.1.call-start = ((), (), s32[]{:S(2)}) async-start(), calls=%async_computation.18 | async-start | bytes 2359296 | tf_op jit(solution)/shard_map/reduce_scatter | solution.py:588
  434.1 9.5 %copy-start.8 = (s32[8,2048]{1,0:T(8,128)S(1)}, s32[8,2048]{1,0:T(8,128)}, u32[]{:S(2)}) copy-start(s32[8,2048]{1,0:T(8,128)} %copy-done.7) | copy-start | bytes 196612
  443.6 1.2 copy-start.12
  444.8 12.9 %copy-start.27 = (f32[256]{0:T(256)S(1)}, f32[256]{0:T(256)}, u32[]{:S(2)}) copy-start(f32[256]{0:T(256)} %param.20) | copy-start | bytes 3076
  450.3 1.0 copy-start.2
  451.3 36.5 %all-to-all-start.2 = ((bf16[8,256,256]{2,1,0:T(8,128)(2,1)}), bf16[8,256,256]{2,1,0:T(8,128)(2,1)S(1)}, u32[]{:S(2)}, u32[]{:S(2)}) async-start(bf16[8,256,256]{2,1,0:T(8,128)(2,1)} %bitcast.71), calls=%async_computation.3 | async-start | bytes 2097152 | tf_op jit(solution)/shard_map/all_to_all | solution.py:513
  480.2 1.0 copy-start.1
  487.7 292.1 %all-to-all-start.3 = ((bf16[8,256,256]{2,1,0:T(8,128)(2,1)}), bf16[8,256,256]{2,1,0:T(8,128)(2,1)}, u32[]{:S(2)}, u32[]{:S(2)}) async-start(bf16[8,256,256]{2,1,0:T(8,128)(2,1)} %bitcast.69), calls=%async_computation.5 | async-start | bytes 2097152 | tf_op jit(solution)/shard_map/all_to_all | solution.py:513
  538.4 236.7 %copy-start.6 = (s32[8,2048]{1,0:T(8,128)S(1)}, s32[8,2048]{1,0:T(8,128)}, u32[]{:S(2)}) copy-start(s32[8,2048]{1,0:T(8,128)} %copy-done.5) | copy-start | bytes 196612
Sparse Core Ops, SparseCore 0:
  11.0 6.1 sort.28.cloned.1.call-done
  63.6 34.1 all-gather.5
  100.4 47.7 all-gather.7
  150.8 47.4 all-gather.11
  200.7 48.6 all-gather.13
  251.4 33.1 all-gather.9
  359.3 44.4 reduce-scatter.10
  406.3 44.3 reduce-scatter.12
  454.7 73.9 reduce-scatter.18
  532.0 64.6 reduce-scatter.14
  600.2 67.1 reduce-scatter.20
  670.8 67.4 reduce-scatter.16
  (1 shorter events, 0.0 us)
